TPU v7x, 32 devices: a whole 2x2x4 slice. The times are simulated.
32 devices in a mesh: dp: 8 (over z, x), tensor: 4 (over y, core).
Axes of the slice: x: 2, y: 2, z: 4, core: 2. Of those that a mesh axis runs over, the one named last changes fastest.
Arguments:
- tokens: bfloat16 [16384, 1536], P(('dp', 'tensor')), may hold values from -6 to 6
- attn_gain: bfloat16 [1536], P('dp'), may hold values from 0.5 to 1.5
- w_query: bfloat16 [1536, 1536], P('dp', 'tensor'), may hold values from -0.15625 to 0.15625
- w_key: bfloat16 [1536, 1536], P('dp', 'tensor'), may hold values from -0.15625 to 0.15625
- w_value: bfloat16 [1536, 1536], P('dp', 'tensor'), may hold values from -0.15625 to 0.15625
- w_outgate: bfloat16 [1536, 1536], P('dp', 'tensor'), may hold values from -0.15625 to 0.15625
- w_forget: bfloat16 [1536, 24], P('dp', 'tensor'), may hold values from -0.15625 to 0.15625
- forget_bias: float32 [24], replicated, may hold values from 0.5 to 7
- w_output: bfloat16 [1536, 1536], P('tensor', 'dp'), may hold values from -0.875 to 0.875
- query_gain: bfloat16 [64], replicated, may hold values from 0.25 to 1.75
- key_gain: bfloat16 [64], replicated, may hold values from 0.25 to 1.75
- mlp_gain: bfloat16 [1536], P('dp'), may hold values from 0.5 to 1.5
- w_gate: bfloat16 [1536, 4096], P('dp', 'tensor'), may hold values from -0.15625 to 0.15625
- w_up: bfloat16 [1536, 4096], P('dp', 'tensor'), may hold values from -0.15625 to 0.15625
- w_down: bfloat16 [4096, 1536], P('tensor', 'dp'), may hold values from -0.125 to 0.125
- lengths: int32 [8], P('dp'), may hold values from 512 to 2048, as said below
- out_grad: bfloat16 [16384, 1536], P(('dp', 'tensor')), may hold values from -6 to 6
Outputs:
- mixed_out: bfloat16 [16384, 1536], P(('dp', 'tensor'))
- tokens_grad: float32 [16384, 1536], P(('dp', 'tensor'))
- attn_gain_grad: float32 [1536], P('dp')
- w_query_grad: float32 [1536, 1536], P('dp', 'tensor')
- w_key_grad: float32 [1536, 1536], P('dp', 'tensor')
- w_value_grad: float32 [1536, 1536], P('dp', 'tensor')
- w_outgate_grad: float32 [1536, 1536], P('dp', 'tensor')
- w_forget_grad: float32 [1536, 24], P('dp', 'tensor')
- forget_bias_grad: float32 [24], replicated
- w_output_grad: float32 [1536, 1536], P('tensor', 'dp')
- query_gain_grad: float32 [64], replicated
- key_gain_grad: float32 [64], replicated
- mlp_gain_grad: float32 [1536], P('dp')
- w_gate_grad: float32 [1536, 4096], P('dp', 'tensor')
- w_up_grad: float32 [1536, 4096], P('dp', 'tensor')
- w_down_grad: float32 [4096, 1536], P('tensor', 'dp')
Inputs may be any that keep to these rules, and one draw needn't show every extreme that they name: `lengths`: in every draw one slot holds exactly 2048 live tokens and another exactly 512.
All inputs are finite; a program needn't handle non-finite values.
Results may differ from a plain program's by a relative error of at most 0.018.
Values may be sent and summed in bfloat16 or wider, within the bound.
A program may use at most 256 MiB of HBM per device.

v0:
```python
import math

import jax
import jax.numpy as jnp
from jax import lax
from jax.sharding import PartitionSpec as P

EPSILON = 1e-05
NEGATIVE = -1e30


def rms_scale(values):
    return lax.rsqrt(jnp.mean(values * values, axis=-1, keepdims=True) + EPSILON)


def norm_backward(values, scaling, grad_normed):
    cubed = scaling * scaling * scaling
    return scaling * grad_normed - values * cubed * jnp.mean(
        grad_normed * values, axis=-1, keepdims=True
    )


def contract_rows(left, right):
    return lax.dot_general(
        left, right, (((0,), (0,)), ((), ())), preferred_element_type=jnp.float32
    )


def times_transpose(left, right):
    return lax.dot_general(
        left, right, (((1,), (1,)), ((), ())), preferred_element_type=jnp.float32
    )


def block_scores(query_low, key_low, cumulative, slot_length, block_start, block_rows):
    slot_size = key_low.shape[0]
    factor = 1.0 / math.sqrt(key_low.shape[2])
    query_block = lax.dynamic_slice_in_dim(query_low, block_start, block_rows, 0)
    cum_block = lax.dynamic_slice_in_dim(cumulative, block_start, block_rows, 0)
    raw_scores = (
        jnp.einsum("qhd,khd->hqk", query_block, key_low, preferred_element_type=jnp.float32)
        * factor
    )
    raw_scores = (
        raw_scores + jnp.transpose(cum_block)[:, :, None] - jnp.transpose(cumulative)[:, None, :]
    )
    key_pos = jnp.arange(slot_size)
    row_pos = block_start + jnp.arange(block_rows)
    allowed = (key_pos[None, :] <= row_pos[:, None]) & (key_pos < slot_length)[None, :]
    return (jnp.where(allowed[None], raw_scores, NEGATIVE), query_block)


def attend_slot(query_low, key_low, value_low, cumulative, slot_length, block_rows):
    slot_size, heads_local, head_dim = query_low.shape

    def forward_block(block_start):
        scores, query_block = block_scores(
            query_low, key_low, cumulative, slot_length, block_start, block_rows
        )
        row_peak = jnp.max(scores, axis=-1, keepdims=True)
        exponent = jnp.exp(scores - row_peak)
        row_total = jnp.sum(exponent, axis=-1, keepdims=True)
        probs_low = (exponent / row_total).astype(jnp.bfloat16)
        attended = jnp.einsum(
            "hqk,khd->qhd", probs_low, value_low, preferred_element_type=jnp.float32
        )
        return (attended, jnp.transpose((row_peak + jnp.log(row_total))[:, :, 0]))

    starts = jnp.arange(slot_size // block_rows) * block_rows
    attended, log_total = lax.map(forward_block, starts)
    return (
        attended.reshape(slot_size, heads_local, head_dim),
        log_total.reshape(slot_size, heads_local),
    )


def attend_slot_back(
    query_low, key_low, value_low, cumulative, log_total, grad_attended, slot_length, block_rows
):
    slot_size, heads_local, head_dim = query_low.shape
    factor = 1.0 / math.sqrt(head_dim)

    def back_block(carried, block_start):
        grad_key, grad_value, grad_cum_keys = carried
        scores, query_block = block_scores(
            query_low, key_low, cumulative, slot_length, block_start, block_rows
        )
        lse_block = lax.dynamic_slice_in_dim(log_total, block_start, block_rows, 0)
        probs = jnp.exp(scores - jnp.transpose(lse_block)[:, :, None])
        probs_low = probs.astype(jnp.bfloat16)
        grad_block = lax.dynamic_slice_in_dim(grad_attended, block_start, block_rows, 0)
        grad_value = grad_value + jnp.einsum(
            "hqk,qhd->khd", probs_low, grad_block, preferred_element_type=jnp.float32
        )
        grad_probs = jnp.einsum(
            "qhd,khd->hqk", grad_block, value_low, preferred_element_type=jnp.float32
        )
        inner = jnp.sum(grad_probs * probs, axis=-1, keepdims=True)
        grad_scores = (probs * (grad_probs - inner)).astype(jnp.bfloat16)
        grad_query = (
            jnp.einsum("hqk,khd->qhd", grad_scores, key_low, preferred_element_type=jnp.float32)
            * factor
        )
        grad_key = (
            grad_key
            + jnp.einsum(
                "hqk,qhd->khd", grad_scores, query_block, preferred_element_type=jnp.float32
            )
            * factor
        )
        scores_float = grad_scores.astype(jnp.float32)
        grad_cum_rows = jnp.transpose(jnp.sum(scores_float, axis=2))
        grad_cum_keys = grad_cum_keys - jnp.transpose(jnp.sum(scores_float, axis=1))
        return ((grad_key, grad_value, grad_cum_keys), (grad_query, grad_cum_rows))

    zeros_heads = jnp.zeros((slot_size, heads_local, head_dim), jnp.float32)
    zeros_cum = jnp.zeros((slot_size, heads_local), jnp.float32)
    starts = jnp.arange(slot_size // block_rows) * block_rows
    carried, stacked = lax.scan(back_block, (zeros_heads, zeros_heads, zeros_cum), starts)
    grad_key, grad_value, grad_cum_keys = carried
    grad_query = stacked[0].reshape(slot_size, heads_local, head_dim)
    grad_cumulative = stacked[1].reshape(slot_size, heads_local) + grad_cum_keys
    return (grad_query, grad_key, grad_value, grad_cumulative)


def per_device(
    tokens,
    attn_gain,
    w_query,
    w_key,
    w_value,
    w_outgate,
    w_forget,
    forget_bias,
    w_output,
    query_gain,
    key_gain,
    mlp_gain,
    w_gate,
    w_up,
    w_down,
    lengths,
    out_grad,
):
    tensor_count = lax.axis_size("tensor")
    tensor_index = lax.axis_index("tensor")
    data_index = lax.axis_index("dp")
    local_rows = tokens.shape[0]
    group_rows = local_rows * tensor_count
    slot_count = lengths.shape[0]
    slot_size = group_rows // slot_count
    heads_local = w_forget.shape[1]
    head_dim = query_gain.shape[0]
    width_local = heads_local * head_dim
    block_rows = min(512, slot_size)
    attn_full = (
        lax.all_gather(attn_gain, "dp", axis=0, tiled=True),
        lax.all_gather(w_query, "dp", axis=0, tiled=True),
        lax.all_gather(w_key, "dp", axis=0, tiled=True),
        lax.all_gather(w_value, "dp", axis=0, tiled=True),
        lax.all_gather(w_outgate, "dp", axis=0, tiled=True),
        lax.all_gather(w_forget, "dp", axis=0, tiled=True),
        lax.all_gather(w_output, "dp", axis=1, tiled=True),
    )
    gain_one, query_full, key_full, value_full, outgate_full, forget_full, output_full = attn_full
    rows_float = tokens.astype(jnp.float32)
    scale_one = rms_scale(rows_float)
    normed_low = (rows_float * scale_one * gain_one.astype(jnp.float32)).astype(jnp.bfloat16)
    normed_all = lax.all_gather(normed_low, "tensor", axis=0, tiled=True)
    query_raw = jnp.dot(normed_all, query_full, preferred_element_type=jnp.float32).reshape(
        group_rows, heads_local, head_dim
    )
    key_raw = jnp.dot(normed_all, key_full, preferred_element_type=jnp.float32).reshape(
        group_rows, heads_local, head_dim
    )
    value_low = jnp.dot(normed_all, value_full, preferred_element_type=jnp.float32).astype(
        jnp.bfloat16
    )
    gate_logit = jnp.dot(normed_all, outgate_full, preferred_element_type=jnp.float32)
    bias_local = lax.dynamic_slice_in_dim(forget_bias, tensor_index * heads_local, heads_local, 0)
    forget_logit = (
        jnp.dot(normed_all, forget_full, preferred_element_type=jnp.float32) + bias_local[None, :]
    )
    query_scale = rms_scale(query_raw)
    key_scale = rms_scale(key_raw)
    query_gain_float = query_gain.astype(jnp.float32)
    key_gain_float = key_gain.astype(jnp.float32)
    query_low = (query_raw * query_scale * query_gain_float).astype(jnp.bfloat16)
    key_low = (key_raw * key_scale * key_gain_float).astype(jnp.bfloat16)
    cumulative = jnp.cumsum(
        jax.nn.log_sigmoid(forget_logit).reshape(slot_count, slot_size, heads_local), axis=1
    )
    slot_query = query_low.reshape(slot_count, slot_size, heads_local, head_dim)
    slot_key = key_low.reshape(slot_count, slot_size, heads_local, head_dim)
    slot_value = value_low.reshape(slot_count, slot_size, heads_local, head_dim)

    def forward_slot(packed):
        return attend_slot(packed[0], packed[1], packed[2], packed[3], packed[4], block_rows)

    attended, log_total = lax.map(
        forward_slot, (slot_query, slot_key, slot_value, cumulative, lengths)
    )
    attended_flat = attended.reshape(group_rows, width_local)
    gate_open = jax.nn.sigmoid(gate_logit)
    gated_low = (attended_flat * gate_open).astype(jnp.bfloat16)
    attn_part = jnp.dot(gated_low, output_full, preferred_element_type=jnp.float32)
    attn_local = lax.psum_scatter(attn_part, "tensor", scatter_dimension=0, tiled=True)
    mixed = rows_float + attn_local
    mlp_full = (
        lax.all_gather(mlp_gain, "dp", axis=0, tiled=True),
        lax.all_gather(w_gate, "dp", axis=0, tiled=True),
        lax.all_gather(w_up, "dp", axis=0, tiled=True),
        lax.all_gather(w_down, "dp", axis=1, tiled=True),
    )
    gain_two, gate_full, up_full, down_full = mlp_full
    scale_two = rms_scale(mixed)
    normed_mid = (mixed * scale_two * gain_two.astype(jnp.float32)).astype(jnp.bfloat16)
    mid_all = lax.all_gather(normed_mid, "tensor", axis=0, tiled=True)
    gate_value = jnp.dot(mid_all, gate_full, preferred_element_type=jnp.float32)
    up_value = jnp.dot(mid_all, up_full, preferred_element_type=jnp.float32)
    gate_sigmoid = jax.nn.sigmoid(gate_value)
    gate_silu = gate_value * gate_sigmoid
    hidden_low = (gate_silu * up_value).astype(jnp.bfloat16)
    mlp_part = jnp.dot(hidden_low, down_full, preferred_element_type=jnp.float32)
    mlp_local = lax.psum_scatter(
        mlp_part.astype(jnp.bfloat16), "tensor", scatter_dimension=0, tiled=True
    ).astype(jnp.float32)
    mixed_out = (mixed + mlp_local).astype(jnp.bfloat16)
    mlp_full = (
        lax.all_gather(mlp_gain, "dp", axis=0, tiled=True),
        lax.all_gather(w_gate, "dp", axis=0, tiled=True),
        lax.all_gather(w_up, "dp", axis=0, tiled=True),
        lax.all_gather(w_down, "dp", axis=1, tiled=True),
    )
    gain_two, gate_full, up_full, down_full = mlp_full
    attn_full = (
        lax.all_gather(attn_gain, "dp", axis=0, tiled=True),
        lax.all_gather(w_query, "dp", axis=0, tiled=True),
        lax.all_gather(w_key, "dp", axis=0, tiled=True),
        lax.all_gather(w_value, "dp", axis=0, tiled=True),
        lax.all_gather(w_outgate, "dp", axis=0, tiled=True),
        lax.all_gather(w_forget, "dp", axis=0, tiled=True),
        lax.all_gather(w_output, "dp", axis=1, tiled=True),
    )
    gain_one, query_full, key_full, value_full, outgate_full, forget_full, output_full = attn_full
    positions = tensor_index * local_rows + jnp.arange(local_rows)
    slot_of_row = positions // slot_size
    row_length = jnp.sum(
        jnp.where(slot_of_row[:, None] == jnp.arange(slot_count)[None, :], lengths[None, :], 0),
        axis=1,
    )
    live_rows = positions % slot_size < row_length
    grad_out = jnp.where(live_rows[:, None], out_grad, jnp.zeros_like(out_grad))
    grad_out_all = lax.all_gather(grad_out, "tensor", axis=0, tiled=True)
    grad_hidden = times_transpose(grad_out_all, down_full)
    grad_down = contract_rows(hidden_low, grad_out_all)
    grad_gate_low = (
        grad_hidden * up_value * gate_sigmoid * (1.0 + gate_value * (1.0 - gate_sigmoid))
    ).astype(jnp.bfloat16)
    grad_up_low = (grad_hidden * gate_silu).astype(jnp.bfloat16)
    grad_gate_w = contract_rows(mid_all, grad_gate_low)
    grad_up_w = contract_rows(mid_all, grad_up_low)
    grad_mid_part = times_transpose(grad_gate_low, gate_full) + times_transpose(
        grad_up_low, up_full
    )
    grad_mid = lax.psum_scatter(grad_mid_part, "tensor", scatter_dimension=0, tiled=True)
    grad_gain_two = jnp.sum(grad_mid * mixed * scale_two, axis=0)
    grad_mixed = grad_out.astype(jnp.float32) + norm_backward(
        mixed, scale_two, grad_mid * gain_two.astype(jnp.float32)
    )
    grad_mixed_low = grad_mixed.astype(jnp.bfloat16)
    grad_mixed_all = lax.all_gather(grad_mixed_low, "tensor", axis=0, tiled=True)
    grad_output_w = contract_rows(gated_low, grad_mixed_all)
    grad_gated = times_transpose(grad_mixed_all, output_full)
    grad_attended_low = (grad_gated * gate_open).astype(jnp.bfloat16)
    grad_gate_logit_low = (grad_gated * attended_flat * gate_open * (1.0 - gate_open)).astype(
        jnp.bfloat16
    )
    grad_outgate_w = contract_rows(normed_all, grad_gate_logit_low)
    slot_grad = grad_attended_low.reshape(slot_count, slot_size, heads_local, head_dim)

    def backward_slot(packed):
        return attend_slot_back(
            packed[0], packed[1], packed[2], packed[3], packed[4], packed[5], packed[6], block_rows
        )

    grad_query_norm, grad_key_norm, grad_value_sum, grad_cumulative = lax.map(
        backward_slot, (slot_query, slot_key, slot_value, cumulative, log_total, slot_grad, lengths)
    )
    grad_log_forget = jnp.flip(jnp.cumsum(jnp.flip(grad_cumulative, 1), axis=1), 1).reshape(
        group_rows, heads_local
    )
    grad_forget_low = (grad_log_forget * jax.nn.sigmoid(-forget_logit)).astype(jnp.bfloat16)
    grad_bias_local = jnp.sum(grad_forget_low.astype(jnp.float32), axis=0)
    grad_forget_w = contract_rows(normed_all, grad_forget_low)
    grad_query_norm = grad_query_norm.reshape(group_rows, heads_local, head_dim)
    grad_key_norm = grad_key_norm.reshape(group_rows, heads_local, head_dim)
    grad_query_gain = jnp.sum(grad_query_norm * query_raw * query_scale, axis=(0, 1))
    grad_key_gain = jnp.sum(grad_key_norm * key_raw * key_scale, axis=(0, 1))
    grad_query_low = (
        norm_backward(query_raw, query_scale, grad_query_norm * query_gain_float)
        .astype(jnp.bfloat16)
        .reshape(group_rows, width_local)
    )
    grad_key_low = (
        norm_backward(key_raw, key_scale, grad_key_norm * key_gain_float)
        .astype(jnp.bfloat16)
        .reshape(group_rows, width_local)
    )
    grad_value_low = grad_value_sum.astype(jnp.bfloat16).reshape(group_rows, width_local)
    grad_query_w = contract_rows(normed_all, grad_query_low)
    grad_key_w = contract_rows(normed_all, grad_key_low)
    grad_value_w = contract_rows(normed_all, grad_value_low)
    grad_normed_part = (
        times_transpose(grad_query_low, query_full)
        + times_transpose(grad_key_low, key_full)
        + times_transpose(grad_value_low, value_full)
        + times_transpose(grad_gate_logit_low, outgate_full)
        + times_transpose(grad_forget_low, forget_full)
    )
    grad_normed = lax.psum_scatter(
        grad_normed_part.astype(jnp.bfloat16), "tensor", scatter_dimension=0, tiled=True
    ).astype(jnp.float32)
    gain_one_float = gain_one.astype(jnp.float32)
    grad_gain_one = jnp.sum(grad_normed * rows_float * scale_one, axis=0)
    tokens_grad = grad_mixed + norm_backward(rows_float, scale_one, grad_normed * gain_one_float)
    bias_spread = lax.dynamic_update_slice_in_dim(
        jnp.zeros(forget_bias.shape, jnp.float32), grad_bias_local, tensor_index * heads_local, 0
    )
    small_sums = lax.psum(
        (grad_gain_one, grad_gain_two, grad_query_gain, grad_key_gain, bias_spread),
        ("dp", "tensor"),
    )
    gain_rows = attn_gain.shape[0]
    attn_gain_grad = lax.dynamic_slice_in_dim(small_sums[0], data_index * gain_rows, gain_rows, 0)
    mlp_gain_grad = lax.dynamic_slice_in_dim(small_sums[1], data_index * gain_rows, gain_rows, 0)
    weight_sums = (
        lax.psum_scatter(
            grad_query_w.astype(jnp.bfloat16), "dp", scatter_dimension=0, tiled=True
        ).astype(jnp.float32),
        lax.psum_scatter(
            grad_key_w.astype(jnp.bfloat16), "dp", scatter_dimension=0, tiled=True
        ).astype(jnp.float32),
        lax.psum_scatter(
            grad_value_w.astype(jnp.bfloat16), "dp", scatter_dimension=0, tiled=True
        ).astype(jnp.float32),
        lax.psum_scatter(
            grad_outgate_w.astype(jnp.bfloat16), "dp", scatter_dimension=0, tiled=True
        ).astype(jnp.float32),
        lax.psum_scatter(
            grad_forget_w.astype(jnp.bfloat16), "dp", scatter_dimension=0, tiled=True
        ).astype(jnp.float32),
        lax.psum_scatter(
            grad_output_w.astype(jnp.bfloat16), "dp", scatter_dimension=1, tiled=True
        ).astype(jnp.float32),
        lax.psum_scatter(
            grad_gate_w.astype(jnp.bfloat16), "dp", scatter_dimension=0, tiled=True
        ).astype(jnp.float32),
        lax.psum_scatter(
            grad_up_w.astype(jnp.bfloat16), "dp", scatter_dimension=0, tiled=True
        ).astype(jnp.float32),
        lax.psum_scatter(
            grad_down.astype(jnp.bfloat16), "dp", scatter_dimension=1, tiled=True
        ).astype(jnp.float32),
    )
    return (
        mixed_out,
        tokens_grad,
        attn_gain_grad,
        weight_sums[0],
        weight_sums[1],
        weight_sums[2],
        weight_sums[3],
        weight_sums[4],
        small_sums[4],
        weight_sums[5],
        small_sums[2],
        small_sums[3],
        mlp_gain_grad,
        weight_sums[6],
        weight_sums[7],
        weight_sums[8],
    )


def solution(mesh):
    in_specs = (
        P(("dp", "tensor"), None),
        P("dp"),
        P("dp", "tensor"),
        P("dp", "tensor"),
        P("dp", "tensor"),
        P("dp", "tensor"),
        P("dp", "tensor"),
        P(),
        P("tensor", "dp"),
        P(),
        P(),
        P("dp"),
        P("dp", "tensor"),
        P("dp", "tensor"),
        P("tensor", "dp"),
        P("dp"),
        P(("dp", "tensor"), None),
    )
    out_specs = (
        P(("dp", "tensor"), None),
        P(("dp", "tensor"), None),
        P("dp"),
        P("dp", "tensor"),
        P("dp", "tensor"),
        P("dp", "tensor"),
        P("dp", "tensor"),
        P("dp", "tensor"),
        P(),
        P("tensor", "dp"),
        P(),
        P(),
        P("dp"),
        P("dp", "tensor"),
        P("dp", "tensor"),
        P("tensor", "dp"),
    )
    return jax.shard_map(
        per_device, mesh=mesh, in_specs=in_specs, out_specs=out_specs, check_vma=False
    )
```

profile of v0, /device:TPU:0, one launch (start us, length us, event | category | flops | bytes accessed | tf_op | source)
XLA Modules:
  0.0 2004.1 jit_solution(2744941091908123866)
XLA Ops:
  13.3 23.9 %all-reduce.3 = (bf16[1536]{0:T(1024)(128)(2,1)S(1)}, bf16[1536]{0:T(1024)(128)(2,1)}) all-reduce(bf16[1536]{0:T(1024)(128)(2,1)S(1)} %dynamic-update-slice, bf16[1536]{0:T(1024)(128)(2,1)S(1)} %dynamic-update-slice.1), channel_id=1, replica_groups=mesh['dp'=8,'tensor'=4] {'dp'}, use_global_device_ids=true, to_apply=%add | all-reduce | flops 3072 | bytes 12288
  44.2 30.6 %all-gather = bf16[8,192,6]{1,2,0:T(8,128)(2,1)S(1)} all-gather(bf16[1,192,6]{1,2,0:T(8,128)(2,1)S(1)} %bitcast.265), channel_id=1, replica_groups=mesh['dp'=8,'tensor'=4] {'dp'}, dimensions={0}, use_global_device_ids=true | all-gather | bytes 20736 | tf_op jit(solution)/shard_map/all_gather | solution.py:162
  92.1 35.9 %all-gather.16.cloned.1.call-done = bf16[1536,384]{1,0:T(8,128)(2,1)} async-done(((bf16[192,384]{1,0:T(8,128)(2,1)}), bf16[1536,384]{1,0:T(8,128)(2,1)}) %all-gather.16.cloned.1.call-update) | async-done | bytes 1179664 | tf_op jit(solution)/shard_map/all_gather | solution.py:158
  134.5 35.5 %all-gather.18.cloned.1.call-done = bf16[1536,384]{1,0:T(8,128)(2,1)} async-done(((bf16[192,384]{1,0:T(8,128)(2,1)}), bf16[1536,384]{1,0:T(8,128)(2,1)}) %all-gather.18.cloned.1.call-update) | async-done | bytes 1179664 | tf_op jit(solution)/shard_map/all_gather | solution.py:159
  180.0 31.9 %all-gather.20.cloned.1.call-done = bf16[1536,384]{1,0:T(8,128)(2,1)} async-done(((bf16[192,384]{1,0:T(8,128)(2,1)}), bf16[1536,384]{1,0:T(8,128)(2,1)}) %all-gather.20.cloned.1.call-update) | async-done | bytes 1179664 | tf_op jit(solution)/shard_map/all_gather | solution.py:160
  217.6 242.1 %while.54 = (s32[]{:T(128)}, f32[4,512,6,64]{1,0,3,2:T(4,128)}, f32[4,512,6]{1,2,0:T(8,128)S(1)}, s32[4]{0:T(128)S(1)}, s32[]{:T(128)}, /*index=5*/bf16[2048,6,6...) while((s32[]{:T(128)}, f32[4,512,6,64]{1,0,3,2:T(4,128)}, ...), condition=%wide.region_8.9_spmd, body=%wide.region_5.8_spmd.sunk | while | flops 1725955584 | bytes 188154064 | solution.py:70
  222.5 13.9 fusion.142
  236.4 14.4 fusion.143
  262.3 16.1 dynamic_update_slice.42
  283.1 13.9 fusion.142
  297.0 14.2 fusion.143
  322.7 16.1 dynamic_update_slice.42
  343.4 13.9 fusion.142
  357.3 14.2 fusion.143
  383.0 16.1 dynamic_update_slice.42
  403.7 13.9 fusion.142
  417.6 14.2 fusion.143
  443.3 16.1 dynamic_update_slice.42
  483.4 97.7 %reduce-scatter.16.cloned.1.call-done = f32[512,1536]{1,0:T(8,128)} async-done(((f32[2048,1536]{1,0:T(8,128)}), f32[512,1536]{1,0:T(8,128)}) %reduce-scatter.16.cloned.1.call-update) | async-done | bytes 3145744 | tf_op jit(solution)/shard_map/reduce_scatter | solution.py:207
  590.2 53.1 %all-gather.30.cloned.1.call-done = bf16[1536,1024]{1,0:T(8,128)(2,1)} async-done(((bf16[192,1024]{1,0:T(8,128)(2,1)}), bf16[1536,1024]{1,0:T(8,128)(2,1)}) %all-gather.30.cloned.1.call-update) | async-done | bytes 3145744 | tf_op jit(solution)/shard_map/all_gather | solution.py:212
  643.3 47.2 %all-gather.26.cloned.1.call-done = bf16[2048,1536]{1,0:T(8,128)(2,1)} async-done(((bf16[512,1536]{1,0:T(8,128)(2,1)}), bf16[2048,1536]{1,0:T(8,128)(2,1)}) %all-gather.26.cloned.1.call-update) | async-done | bytes 6291472 | tf_op jit(solution)/shard_map/all_gather | solution.py:218
  690.5 11.6 fusion.55
  702.1 50.5 %all-gather.28.cloned.1.call-done = bf16[1536,1024]{1,0:T(8,128)(2,1)} async-done(((bf16[192,1024]{1,0:T(8,128)(2,1)}), bf16[1536,1024]{1,0:T(8,128)(2,1)}) %all-gather.28.cloned.1.call-update) | async-done | bytes 3145744 | tf_op jit(solution)/shard_map/all_gather | solution.py:211
  752.6 11.7 fusion.54
  764.3 49.2 %all-gather.32.cloned.1.call-done = bf16[1024,1536]{0,1:T(8,128)(2,1)} async-done(((bf16[1024,192]{0,1:T(8,128)(2,1)}), bf16[1024,1536]{0,1:T(8,128)(2,1)}) %all-gather.32.cloned.1.call-update) | async-done | bytes 3145744 | tf_op jit(solution)/shard_map/all_gather | solution.py:213
  813.5 46.5 %all-gather.34.cloned.1.call-done = bf16[2048,1536]{1,0:T(8,128)(2,1)} async-done(((bf16[512,1536]{1,0:T(8,128)(2,1)}), bf16[2048,1536]{1,0:T(8,128)(2,1)}) %all-gather.34.cloned.1.call-update) | async-done | bytes 6291472 | tf_op jit(solution)/shard_map/all_gather | solution.py:254
  859.9 18.2 multiply_convert_fusion.1
  887.9 12.9 convolution_add_fusion
  900.8 12.1 convolution_convert_fusion
  913.0 87.6 %reduce-scatter.20.cloned.1.call-done = f32[512,1536]{1,0:T(8,128)} async-done(((f32[2048,1536]{1,0:T(8,128)}), f32[512,1536]{1,0:T(8,128)}) %reduce-scatter.20.cloned.1.call-update) | async-done | bytes 3145744 | tf_op jit(solution)/shard_map/reduce_scatter | solution.py:266
  1003.8 58.0 %reduce-scatter.18.cloned.1.call-done = bf16[512,1536]{1,0:T(8,128)(2,1)} async-done(((bf16[2048,1536]{1,0:T(8,128)(2,1)}), bf16[512,1536]{1,0:T(8,128)(2,1)}) %reduce-scatter.18.cloned.1.call-update) | async-done | bytes 1572880 | tf_op jit(solution)/shard_map/reduce_scatter | solution.py:225
  1067.1 11.3 convolution_convert_fusion.1
  1078.5 11.7 convolution_convert_fusion.2
  1090.3 11.3 convolution_convert_fusion.3
  1101.7 11.9 all-gather.36.cloned.1.call-done
  1123.4 358.4 %while.55 = (s32[]{:T(128)}, f32[2048,6,64]{0,2,1:T(8,128)S(1)}, f32[2048,6,64]{0,2,1:T(8,128)}, f32[2048,6]{0,1:T(8,128)S(1)}, f32[4,512,6,64]{1,3,2,0:T(8,128)...) while((s32[]{:T(128)}, f32[2048,6,64]{0,2,1:T(8,128)S(1)}, ...), condition=%wide.region_18.19_spmd.clone, body=%wide.region_14.18_spmd.clone.sunk | while | flops 4120846848 | bytes 261230864 | solution.py:119
  1129.0 14.9 subtract_exponential_fusion.3
  1144.0 12.6 bitcast_add_fusion.5
  1156.6 21.2 %multiply_reduce_fusion.10 = (f32[6,512]{1,0:T(8,128)S(1)}, f32[6,512,2048]{2,1,0:T(8,128)}) fusion(f32[6,512,2048]{2,1,0:T(8,128)} %subtract_exponential_fusion.3, bf16[2048,6,64]{0,2,1:T(8,128)(2,1)} %get-tuple-element.594, bf16[2048,6,64]{0,2,1:T(8,128)(2,1)} %get-tuple-element.593, s32[]{:T(128)S(6)} %select_n.115), kind=kOutput, calls=%fused_computation.21.clone.1 | convolution fusion | flops 817886208 | bytes 52310020 | tf_op jit(solution)/shard_map/while/body/eval_jaxpr/while/body/eval_jaxpr/qhd,khd->hqk/dot_general | solution.py:95
  1177.8 16.8 convert_reduce_fusion.4
  1203.0 9.9 fusion.155
  1218.2 14.9 subtract_exponential_fusion.3
  1233.2 13.5 bitcast_add_fusion.5
  1246.7 21.2 %multiply_reduce_fusion.10 = (f32[6,512]{1,0:T(8,128)S(1)}, f32[6,512,2048]{2,1,0:T(8,128)}) fusion(f32[6,512,2048]{2,1,0:T(8,128)} %subtract_exponential_fusion.3, bf16[2048,6,64]{0,2,1:T(8,128)(2,1)} %get-tuple-element.594, bf16[2048,6,64]{0,2,1:T(8,128)(2,1)} %get-tuple-element.593, s32[]{:T(128)S(6)} %select_n.115), kind=kOutput, calls=%fused_computation.21.clone.1 | convolution fusion | flops 817886208 | bytes 52310020 | tf_op jit(solution)/shard_map/while/body/eval_jaxpr/while/body/eval_jaxpr/qhd,khd->hqk/dot_general | solution.py:95
  1267.9 16.7 convert_reduce_fusion.4
  1293.0 10.1 fusion.155
  1308.5 14.9 subtract_exponential_fusion.3
  1323.5 13.6 bitcast_add_fusion.5
  1337.0 20.9 %multiply_reduce_fusion.10 = (f32[6,512]{1,0:T(8,128)S(1)}, f32[6,512,2048]{2,1,0:T(8,128)}) fusion(f32[6,512,2048]{2,1,0:T(8,128)} %subtract_exponential_fusion.3, bf16[2048,6,64]{0,2,1:T(8,128)(2,1)} %get-tuple-element.594, bf16[2048,6,64]{0,2,1:T(8,128)(2,1)} %get-tuple-element.593, s32[]{:T(128)S(6)} %select_n.115), kind=kOutput, calls=%fused_computation.21.clone.1 | convolution fusion | flops 817886208 | bytes 52310020 | tf_op jit(solution)/shard_map/while/body/eval_jaxpr/while/body/eval_jaxpr/qhd,khd->hqk/dot_general | solution.py:95
  1357.9 16.4 convert_reduce_fusion.4
  1398.0 14.9 subtract_exponential_fusion.3
  1412.9 13.2 bitcast_add_fusion.5
  1426.1 20.6 %multiply_reduce_fusion.10 = (f32[6,512]{1,0:T(8,128)S(1)}, f32[6,512,2048]{2,1,0:T(8,128)}) fusion(f32[6,512,2048]{2,1,0:T(8,128)} %subtract_exponential_fusion.3, bf16[2048,6,64]{0,2,1:T(8,128)(2,1)} %get-tuple-element.594, bf16[2048,6,64]{0,2,1:T(8,128)(2,1)} %get-tuple-element.593, s32[]{:T(128)S(6)} %select_n.115), kind=kOutput, calls=%fused_computation.21.clone.1 | convolution fusion | flops 817886208 | bytes 52310020 | tf_op jit(solution)/shard_map/while/body/eval_jaxpr/while/body/eval_jaxpr/qhd,khd->hqk/dot_general | solution.py:95
  1446.8 16.4 convert_reduce_fusion.4
  1471.6 9.8 fusion.155
  1539.7 10.0 fusion.57
  1569.4 19.8 add_convert_fusion
  1604.5 16.2 reduce-scatter.32.cloned.1.call-done
  1622.3 65.4 %reduce-scatter.26.cloned.1.call-done = bf16[192,384]{1,0:T(8,128)(2,1)} async-done(((bf16[1536,384]{1,0:T(8,128)(2,1)}), bf16[192,384]{1,0:T(8,128)(2,1)}) %reduce-scatter.26.cloned.1.call-update) | async-done | bytes 147472 | tf_op jit(solution)/shard_map/reduce_scatter | solution.py:341
  1689.4 65.4 %reduce-scatter.30.cloned.1.call-done = bf16[192,384]{1,0:T(8,128)(2,1)} async-done(((bf16[1536,384]{1,0:T(8,128)(2,1)}), bf16[192,384]{1,0:T(8,128)(2,1)}) %reduce-scatter.30.cloned.1.call-update) | async-done | bytes 147472 | tf_op jit(solution)/shard_map/reduce_scatter | solution.py:347
  1756.4 65.4 %reduce-scatter.28.cloned.1.call-done = bf16[192,384]{1,0:T(8,128)(2,1)} async-done(((bf16[1536,384]{1,0:T(8,128)(2,1)}), bf16[192,384]{1,0:T(8,128)(2,1)}) %reduce-scatter.28.cloned.1.call-update) | async-done | bytes 147472 | tf_op jit(solution)/shard_map/reduce_scatter | solution.py:344
  1823.5 65.4 %reduce-scatter.24.cloned.1.call-done = bf16[192,384]{1,0:T(8,128)(2,1)} async-done(((bf16[1536,384]{1,0:T(8,128)(2,1)}), bf16[192,384]{1,0:T(8,128)(2,1)}) %reduce-scatter.24.cloned.1.call-update) | async-done | bytes 147472 | tf_op jit(solution)/shard_map/reduce_scatter | solution.py:338
  1890.5 58.7 %reduce-scatter.22.cloned.1.call-done = bf16[512,1536]{1,0:T(8,128)(2,1)} async-done(((bf16[2048,1536]{1,0:T(8,128)(2,1)}), bf16[512,1536]{1,0:T(8,128)(2,1)}) %reduce-scatter.22.cloned.1.call-update) | async-done | bytes 1572880 | tf_op jit(solution)/shard_map/reduce_scatter | solution.py:321
  1951.9 39.7 %all-reduce.2 = (f32[1536]{0:T(1024)S(1)}, f32[24]{0:T(128)}, f32[64]{0:T(128)}, f32[64]{0:T(128)}, f32[1536]{0:T(1024)S(1)}) all-reduce(f32[1536]{0:T(1024)S(1)} %get-tuple-element.267, f32[24]{0:T(128)S(1)} %dynamic_update_slice.31, f32[64]{0:T(128)S(1)} %fusion.40, ...), channel_id=1, replica_groups=mesh['dp'=8,'tensor'=4] {'dp','tensor'}, use_global_device_ids=true, to_apply=%region_26.27 | all-reduce | flops 3224 | bytes 25792 | tf_op jit(solution)/shard_map/psum | solution.py:330
  (363 shorter events, 334.8 us)
Async XLA Ops:
  7.2 77.4 %all-gather.14.cloned.1.call-start = ((), (), s32[]{:S(2)}) async-start(), calls=%async_computation.13 | async-start | bytes 7864320 | tf_op jit(solution)/shard_map/all_gather | solution.py:169
  9.0 35.1 %copy-start.50 = (bf16[64]{0:T(256)(128)(2,1)S(1)}, bf16[64]{0:T(256)(128)(2,1)}, u32[]{:S(2)}) copy-start(bf16[64]{0:T(256)(128)(2,1)} %param.31) | copy-start | bytes 388
  9.0 35.1 %copy-start.46 = (bf16[64]{0:T(256)(128)(2,1)S(1)}, bf16[64]{0:T(256)(128)(2,1)}, u32[]{:S(2)}) copy-start(bf16[64]{0:T(256)(128)(2,1)} %param.30) | copy-start | bytes 388
  9.0 35.1 %copy-start.42 = (bf16[192,6]{0,1:T(8,128)(2,1)S(1)}, bf16[192,6]{0,1:T(8,128)(2,1)}, u32[]{:S(2)}) copy-start(bf16[192,6]{0,1:T(8,128)(2,1)} %param.27) | copy-start | bytes 6916
  9.1 65.9 %copy-start.51 = (f32[24]{0:T(128)S(1)}, f32[24]{0:T(128)}, u32[]{:S(2)}) copy-start(f32[24]{0:T(128)} %param.28) | copy-start | bytes 292
  9.7 65.1 %copy-start.37 = (f32[512]{0:T(512)}, f32[512]{0:T(512)S(1)}, u32[]{:S(2)}) copy-start(f32[512]{0:T(512)S(1)} %get-tuple-element.346) | copy-start | bytes 6148
  40.8 87.1 %all-gather.16.cloned.1.call-start = ((), (), s32[]{:S(2)}) async-start(), calls=%async_computation.14 | async-start | bytes 1327104 | tf_op jit(solution)/shard_map/all_gather | solution.py:158
  41.6 128.4 %all-gather.18.cloned.1.call-start = ((), (), s32[]{:S(2)}) async-start(), calls=%async_computation.15 | async-start | bytes 1327104 | tf_op jit(solution)/shard_map/all_gather | solution.py:159
  42.3 169.6 %all-gather.20.cloned.1.call-start = ((), (), s32[]{:S(2)}) async-start(), calls=%async_computation.16 | async-start | bytes 1327104 | tf_op jit(solution)/shard_map/all_gather | solution.py:160
  42.9 422.6 %all-gather.22.cloned.1.call-start = ((), (), s32[]{:S(2)}) async-start(), calls=%async_computation.17 | async-start | bytes 1327104 | tf_op jit(solution)/shard_map/all_gather | solution.py:161
  43.5 430.8 %all-gather.24.cloned.1.call-start = ((), (), s32[]{:S(2)}) async-start(), calls=%async_computation.18 | async-start | bytes 1327104 | tf_op jit(solution)/shard_map/all_gather | solution.py:163
  44.1 537.0 %reduce-scatter.16.cloned.1.call-start = ((), (), s32[]{:S(2)}) async-start(), calls=%async_computation.19 | async-start | bytes 15728640 | tf_op jit(solution)/shard_map/reduce_scatter | solution.py:207
  44.2 132.4 %copy-start.40 = (f32[64]{0:T(128)}, f32[64]{0:T(128)S(1)}, u32[]{:S(2)}) copy-start(f32[64]{0:T(128)S(1)} %convert_element_type.159) | copy-start | bytes 772
  44.2 132.4 %copy-start.44 = (f32[64]{0:T(128)}, f32[64]{0:T(128)S(1)}, u32[]{:S(2)}) copy-start(f32[64]{0:T(128)S(1)} %convert_element_type.157) | copy-start | bytes 772
  74.9 14.2 copy-start.32
  133.1 43.5 %copy-start.2 = (f32[2048,384]{0,1:T(8,128)}, f32[2048,384]{0,1:T(8,128)S(1)}, u32[]{:S(2)}) copy-start(f32[2048,384]{0,1:T(8,128)S(1)} %fusion.51) | copy-start | bytes 9437188
  134.5 42.1 %copy-start.23 = (f32[2048,6]{0,1:T(8,128)}, f32[2048,6]{0,1:T(8,128)S(1)}, u32[]{:S(2)}) copy-start(f32[2048,6]{0,1:T(8,128)S(1)} %get-tuple-element.344) | copy-start | bytes 147460
  236.4 15.8 copy-start.1
  297.0 15.5 copy-start.1
  357.3 15.5 copy-start.1
  417.6 15.5 copy-start.1
  474.3 8.2 copy-start.17
  482.6 160.7 %all-gather.30.cloned.1.call-start = ((), (), s32[]{:S(2)}) async-start(), calls=%async_computation.22 | async-start | bytes 3538944 | tf_op jit(solution)/shard_map/all_gather | solution.py:212
  483.3 207.2 %all-gather.26.cloned.1.call-start = ((), (), s32[]{:S(2)}) async-start(), calls=%async_computation.20 | async-start | bytes 7864320 | tf_op jit(solution)/shard_map/all_gather | solution.py:218
  585.4 167.2 %all-gather.28.cloned.1.call-start = ((), (), s32[]{:S(2)}) async-start(), calls=%async_computation.21 | async-start | bytes 3538944 | tf_op jit(solution)/shard_map/all_gather | solution.py:211
  586.0 227.5 %all-gather.32.cloned.1.call-start = ((), (), s32[]{:S(2)}) async-start(), calls=%async_computation.23 | async-start | bytes 3538944 | tf_op jit(solution)/shard_map/all_gather | solution.py:213
  586.7 273.2 %all-gather.34.cloned.1.call-start = ((), (), s32[]{:S(2)}) async-start(), calls=%async_computation.25 | async-start | bytes 7864320 | tf_op jit(solution)/shard_map/all_gather | solution.py:254
  590.2 410.4 %reduce-scatter.20.cloned.1.call-start = ((), (), s32[]{:S(2)}) async-start(), calls=%async_computation.26 | async-start | bytes 15728640 | tf_op jit(solution)/shard_map/reduce_scatter | solution.py:266
  859.9 18.2 copy-start.49
  878.2 9.7 copy-start.54
  878.2 9.7 copy-start.48
  878.2 9.7 copy-start.55
  900.8 161.1 %reduce-scatter.18.cloned.1.call-start = ((), (), s32[]{:S(2)}) async-start(), calls=%async_computation.24 | async-start | bytes 7864320 | tf_op jit(solution)/shard_map/reduce_scatter | solution.py:225
  912.9 200.7 %all-gather.36.cloned.1.call-start = ((), (), s32[]{:S(2)}) async-start(), calls=%async_computation.27 | async-start | bytes 7864320 | tf_op jit(solution)/shard_map/all_gather | solution.py:272
  1067.1 525.6 %reduce-scatter.38.cloned.1.call-start = ((), (), s32[]{:S(2)}) async-start(), calls=%async_computation.36 | async-start | bytes 3538944 | tf_op jit(solution)/shard_map/reduce_scatter | solution.py:362
  1078.5 516.2 %reduce-scatter.36.cloned.1.call-start = ((), (), s32[]{:S(2)}) async-start(), calls=%async_computation.35 | async-start | bytes 3538944 | tf_op jit(solution)/shard_map/reduce_scatter | solution.py:359
  1090.2 506.4 %reduce-scatter.34.cloned.1.call-start = ((), (), s32[]{:S(2)}) async-start(), calls=%async_computation.34 | async-start | bytes 3538944 | tf_op jit(solution)/shard_map/reduce_scatter | solution.py:356
  1101.7 501.3 %reduce-scatter.40.cloned.1.call-start = ((), (), s32[]{:S(2)}) async-start(), calls=%async_computation.37 | async-start | bytes 442368
  1113.6 9.8 copy-start.16
  1113.6 9.8 copy-start.53
  1123.4 362.9 %copy-start.28 = (f32[2048,6]{0,1:T(8,128)S(1)}, f32[2048,6]{0,1:T(8,128)}, u32[]{:S(2)}) copy-start(f32[2048,6]{0,1:T(8,128)} %copy-done.27) | copy-start | bytes 147460
  1491.2 8.0 copy-start.26
  1491.2 8.0 copy-start.41
  1491.2 129.5 %reduce-scatter.32.cloned.1.call-start = ((), (), s32[]{:S(2)}) async-start(), calls=%async_computation.33 | async-start | bytes 1327104 | tf_op jit(solution)/shard_map/reduce_scatter | solution.py:353
  1499.1 188.6 %reduce-scatter.26.cloned.1.call-start = ((), (), s32[]{:S(2)}) async-start(), calls=%async_computation.30 | async-start | bytes 1327104 | tf_op jit(solution)/shard_map/reduce_scatter | solution.py:341
  1508.8 245.9 %reduce-scatter.30.cloned.1.call-start = ((), (), s32[]{:S(2)}) async-start(), calls=%async_computation.32 | async-start | bytes 1327104 | tf_op jit(solution)/shard_map/reduce_scatter | solution.py:347
  1516.3 305.5 %reduce-scatter.28.cloned.1.call-start = ((), (), s32[]{:S(2)}) async-start(), calls=%async_computation.31 | async-start | bytes 1327104 | tf_op jit(solution)/shard_map/reduce_scatter | solution.py:344
  1519.6 7.7 copy-start.47
  1519.6 7.8 copy-start.8
  1527.1 361.7 %reduce-scatter.24.cloned.1.call-start = ((), (), s32[]{:S(2)}) async-start(), calls=%async_computation.29 | async-start | bytes 1327104 | tf_op jit(solution)/shard_map/reduce_scatter | solution.py:338
  1539.6 409.6 %reduce-scatter.22.cloned.1.call-start = ((), (), s32[]{:S(2)}) async-start(), calls=%async_computation.28 | async-start | bytes 7864320 | tf_op jit(solution)/shard_map/reduce_scatter | solution.py:321
  1539.6 10.0 copy-start.10
  1539.6 10.0 copy-start.21
  1549.6 6.8 copy-start.19
  1549.6 6.8 copy-start.22
  1556.4 6.5 copy-start.13
  1556.4 6.5 copy-start.20
  1562.9 6.5 copy-start.33
  1598.7 350.5 %copy-start.7 = (bf16[512,1536]{1,0:T(8,128)(2,1)S(1)}, bf16[512,1536]{1,0:T(8,128)(2,1)}, u32[]{:S(2)}) copy-start(bf16[512,1536]{1,0:T(8,128)(2,1)} %param.21) | copy-start | bytes 4718596
  1598.7 350.5 %copy-start.35 = (f32[1536]{0:T(1024)S(1)}, f32[1536]{0:T(1024)}, u32[]{:S(2)}) copy-start(f32[1536]{0:T(1024)} %copy-done.34) | copy-start | bytes 18436
  1598.7 350.5 %copy-start.38 = (f32[512]{0:T(512)S(1)}, f32[512]{0:T(512)}, u32[]{:S(2)}) copy-start(f32[512]{0:T(512)} %copy-done.37) | copy-start | bytes 6148
  1602.9 349.0 %copy-start.36 = (f32[1536]{0:T(1024)S(1)}, f32[1536]{0:T(1024)}, u32[]{:S(2)}) copy-start(f32[1536]{0:T(1024)} %get-tuple-element.263) | copy-start | bytes 18436
  1602.9 390.0 %copy-start.39 = (f32[512]{0:T(512)S(1)}, f32[512]{0:T(512)}, u32[]{:S(2)}) copy-start(f32[512]{0:T(512)} %get-tuple-element.345) | copy-start | bytes 6148
  1949.2 43.7 %copy-start.14 = (bf16[512,1536]{1,0:T(8,128)(2,1)S(1)}, bf16[512,1536]{1,0:T(8,128)(2,1)}, u32[]{:S(2)}) copy-start(bf16[512,1536]{1,0:T(8,128)(2,1)} %reduce-scatter.22.cloned.1.call-done) | copy-start | bytes 4718596
  (27 other events, 77.5 us)
Sparse Core Ops, SparseCore 0:
  40.9 43.6 all-gather.13
  86.8 41.1 all-gather.15
  130.1 39.8 all-gather.17
  172.0 39.8 all-gather.19
  213.9 39.8 all-gather.21
  255.8 39.8 all-gather.23
  482.7 98.3 reduce-scatter.15
  583.2 60.0 all-gather.29
  645.4 45.0 all-gather.25
  692.5 60.0 all-gather.27
  754.7 58.6 all-gather.31
  814.9 45.0 all-gather.33
  900.9 99.6 reduce-scatter.19
  1003.0 58.8 reduce-scatter.17
  1067.2 46.3 all-gather.35
  1117.0 74.2 reduce-scatter.37
  1194.8 73.4 reduce-scatter.35
  1271.6 73.4 reduce-scatter.33
  1491.3 62.1 reduce-scatter.39
  1556.8 63.8 reduce-scatter.31
  1624.1 63.5 reduce-scatter.25
  1691.1 63.6 reduce-scatter.29
  1758.2 63.5 reduce-scatter.27
  1825.1 63.7 reduce-scatter.23
  1891.4 57.7 reduce-scatter.21
where the time goes:
time: 2020 us; the launch traced here: 2000 us
  waiting for transfers between devices  956 us (47%)
  matrix products  587 us (29%)
  other arithmetic  204 us (10%)
  local copies, waits for them, and re-layouts  127 us (6%)
  blocking collectives  94.3 us (5%)
    dot_general x8, matrix products, block_scores(): jnp.einsum('qhd,khd->hqk', query_block, key_low, preferred_element_type=j...  115 us
    dot_general x9, matrix products, times_transpose(): lax.dot_general(left, right, (((1,), (1,)), ((), ())), preferred_element_...  100 us
    reduce_scatter x1, waiting for transfers between devices, per_device(): lax.psum_scatter(attn_part, 'tensor', scatter_dimension=0, tiled=True)  97.7 us
    reduce_scatter x1, waiting for transfers between devices, per_device(): lax.psum_scatter(grad_mid_part, 'tensor', scatter_dimension=0, tiled=True)  87.6 us
    dot_general x4, matrix products, back_block(): jnp.einsum('qhd,khd->hqk', grad_block, value_low, preferred_element_type=...  83.9 us
    dot_general x9, matrix products, contract_rows(): lax.dot_general(left, right, (((0,), (0,)), ((), ())), preferred_element_...  69.9 us
    dynamic_update_slice x12, local copies, waits for them, and re-layouts, attend_slot(): attended, log_total = lax.map(forward_block, starts)  67.5 us
    reduce_sum x4, other arithmetic, back_block(): grad_cum_rows = jnp.transpose(jnp.sum(scores_float, axis=2))  66.4 us
  transfers between devices with their start and end apart: 25, of which 19 were waited for; matrix products, arithmetic and copies ran while one was open for 41% of the time, Pallas kernels for 0%

commit v1 on v0

v1 whole, which is shorter than its diff:
```python
import functools
import math

import jax
import jax.numpy as jnp
from jax import lax
from jax.experimental import pallas as pl
from jax.experimental.pallas import tpu as pltpu
from jax.sharding import PartitionSpec as P

NEGATIVE = -1e30
EPSILON = 1e-05


def nt(left, right):
    return lax.dot_general(
        left, right, (((1,), (1,)), ((), ())), preferred_element_type=jnp.float32
    )


def tn(left, right):
    return lax.dot_general(
        left, right, (((0,), (0,)), ((), ())), preferred_element_type=jnp.float32
    )


def nn(left, right):
    return jnp.dot(left, right, preferred_element_type=jnp.float32)


def split_three(values):
    high = values.astype(jnp.bfloat16).astype(jnp.float32)
    rest = values - high
    middle = rest.astype(jnp.bfloat16).astype(jnp.float32)
    return high, middle, rest - middle


def placed_pieces(values, lane, first):
    high, middle, low = split_three(values)
    return jnp.where(
        lane == first, high, jnp.where(lane == first + 1, middle, jnp.where(lane == first + 2, low, 0.0))
    )


def turned(values, head, half):
    return values if head == 0 else pltpu.roll(values, half, 1)


def attend_kernel(
    heads, half, block, x_ref, cq_ref, ck_ref, qg_ref, kg_ref, att_ref, qb_ref, kf_ref, qf, vf
):
    pair = pl.program_id(0)
    slot = x_ref.shape[0]
    wide = 2 * half
    blocks = slot // block
    lane = lax.broadcasted_iota(jnp.int32, (block, wide), 1)
    lower = lane < half
    row = lax.broadcasted_iota(jnp.int32, (wide, wide), 0)
    col = lax.broadcasted_iota(jnp.int32, (wide, wide), 1)
    below = lax.broadcasted_iota(jnp.int32, (block, block), 0) >= lax.broadcasted_iota(
        jnp.int32, (block, block), 1
    )
    for h in range(2):
        head = pair * 2 + h
        place_q = ((row == (col - half) * heads + head) & (col >= half) & (col < half + 3)).astype(
            jnp.bfloat16
        )
        place_k = (
            (row == (col - half - 3) * heads + head) & (col >= half + 3) & (col < half + 6)
        ).astype(jnp.bfloat16)

        def prepare(b, _):
            rows = pl.ds(pl.multiple_of(b * block, block), block)
            q = turned(x_ref[rows, 0:wide], h, half)
            k = turned(x_ref[rows, wide : 2 * wide], h, half)
            v = turned(x_ref[rows, 2 * wide : 3 * wide], h, half)
            q_scale = lax.rsqrt(
                jnp.sum(jnp.where(lower, q * q, 0.0), axis=1, keepdims=True) / half + EPSILON
            )
            k_scale = lax.rsqrt(
                jnp.sum(jnp.where(lower, k * k, 0.0), axis=1, keepdims=True) / half + EPSILON
            )
            q_low = (q * q_scale * qg_ref[...]).astype(jnp.bfloat16).astype(jnp.float32)
            k_low = k * k_scale * kg_ref[...]
            q_bias = nn(cq_ref[rows, :], place_q) + jnp.where(
                (lane >= half + 3) & (lane < half + 6), 1.0, 0.0
            )
            k_bias = nn(ck_ref[rows, :], place_k) + jnp.where(
                (lane >= half) & (lane < half + 3), 1.0, 0.0
            )
            qf[rows, :] = jnp.where(lower, q_low * (1.0 / math.sqrt(half)), q_bias).astype(
                jnp.bfloat16
            )
            kf_ref[h, rows, :] = jnp.where(lower, k_low, k_bias).astype(jnp.bfloat16)
            vf[rows, :] = jnp.where(lower, v, 1.0).astype(jnp.bfloat16)
            return 0

        lax.fori_loop(0, blocks, prepare, 0)
        for qb in range(blocks):
            rows = pl.ds(qb * block, block)
            query = qf[rows, :]
            total = jnp.zeros((block, wide), jnp.float32)
            for kb in range(qb + 1):
                keys = pl.ds(kb * block, block)
                scores = nt(query, kf_ref[h, keys, :])
                if kb == qb:
                    scores = jnp.where(below, scores, NEGATIVE)
                total = total + nn(jnp.exp(scores).astype(jnp.bfloat16), vf[keys, :])
            out = total / pltpu.roll(total, half, 1)
            if h == 0:
                att_ref[rows, :] = out
            else:
                att_ref[rows, :] = jnp.where(lower, att_ref[rows, :], pltpu.roll(out, half, 1))
            query_float = query.astype(jnp.float32)
            bias = jnp.sum(
                jnp.where((lane >= half) & (lane < half + 3), query_float, 0.0),
                axis=1,
                keepdims=True,
            )
            shifted = bias - jnp.log(jnp.where(lower, 1.0, total))
            qb_ref[h, rows, :] = jnp.where(
                (lane >= half) & (lane < half + 3),
                placed_pieces(shifted, lane, half),
                query_float,
            ).astype(jnp.bfloat16)


def attend_back_kernel(
    half,
    block,
    x_ref,
    qb_ref,
    kf_ref,
    att_ref,
    do_ref,
    qg_ref,
    kg_ref,
    grad_ref,
    cum_ref,
    gain_ref,
    vf,
    dof,
    key_turned,
    dq_turned,
    dk_all,
    dv_all,
):
    pair = pl.program_id(0)
    slot = x_ref.shape[0]
    wide = 2 * half
    blocks = slot // block
    lane = lax.broadcasted_iota(jnp.int32, (block, wide), 1)
    lower = lane < half
    above = lax.broadcasted_iota(jnp.int32, (block, block), 0) <= lax.broadcasted_iota(
        jnp.int32, (block, block), 1
    )

    @pl.when(pair == 0)
    def _():
        gain_ref[...] = jnp.zeros_like(gain_ref)
        cum_ref[...] = jnp.zeros_like(cum_ref)

    for h in range(2):
        head = pair * 2 + h

        def prepare(b, _):
            rows = pl.ds(pl.multiple_of(b * block, block), block)
            v = turned(x_ref[rows, 2 * wide : 3 * wide], h, half)
            grad = turned(do_ref[rows, :].astype(jnp.float32), h, half)
            out = turned(att_ref[rows, :], h, half)
            inner = jnp.sum(jnp.where(lower, grad * out, 0.0), axis=1, keepdims=True)
            vf[rows, :] = jnp.where(lower, v, 1.0).astype(jnp.bfloat16)
            dof[rows, :] = jnp.where(lower, grad, placed_pieces(-inner, lane, half)).astype(
                jnp.bfloat16
            )
            key_turned[:, rows] = kf_ref[h, rows, :].astype(jnp.float32).T.astype(jnp.bfloat16)
            return 0

        lax.fori_loop(0, blocks, prepare, 0)
        for kb in range(blocks):
            keys = pl.ds(kb * block, block)
            key = kf_ref[h, keys, :]
            value = vf[keys, :]
            dk = jnp.zeros((block, wide), jnp.float32)
            dv = jnp.zeros((block, wide), jnp.float32)
            for qb in range(kb, blocks):
                rows = pl.ds(qb * block, block)
                query = qb_ref[h, rows, :]
                grad = dof[rows, :]
                scores = nt(key, query)
                if kb == qb:
                    scores = jnp.where(above, scores, NEGATIVE)
                probs = jnp.exp(scores)
                dv = dv + nn(probs.astype(jnp.bfloat16), grad)
                grad_scores = (probs * nt(value, grad)).astype(jnp.bfloat16)
                dk = dk + nn(grad_scores, query)
                part = nn(key_turned[:, keys], grad_scores)
                if kb == 0:
                    dq_turned[:, rows] = part
                else:
                    dq_turned[:, rows] += part
            dk_all[keys, :] = dk
            dv_all[keys, :] = dv

        def finish(b, sums):
            rows = pl.ds(pl.multiple_of(b * block, block), block)
            dq = dq_turned[:, rows].T
            dk = dk_all[rows, :]
            change = jnp.sum(
                jnp.where(lane == half, dq - pltpu.roll(dk, wide - 3, 1), 0.0),
                axis=1,
                keepdims=True,
            )
            cum_ref[rows, :] = jnp.where(lane == head, change, cum_ref[rows, :])

            def one(raw, grad, gain):
                scale = lax.rsqrt(
                    jnp.sum(jnp.where(lower, raw * raw, 0.0), axis=1, keepdims=True) / half
                    + EPSILON
                )
                inward = grad * gain
                mean = (
                    jnp.sum(jnp.where(lower, inward * raw, 0.0), axis=1, keepdims=True) / half
                )
                out = scale * inward - raw * (scale * scale * scale) * mean
                return out, jnp.sum(grad * raw * scale, axis=0, keepdims=True)

            q_out, q_sum = one(
                turned(x_ref[rows, 0:wide], h, half), dq * (1.0 / math.sqrt(half)), qg_ref[...]
            )
            k_out, k_sum = one(turned(x_ref[rows, wide : 2 * wide], h, half), dk, kg_ref[...])
            v_out = dv_all[rows, :]
            for i, out in enumerate((q_out, k_out, v_out)):
                at = slice(i * wide, (i + 1) * wide)
                if h == 0:
                    grad_ref[rows, at] = out.astype(jnp.bfloat16)
                else:
                    grad_ref[rows, at] = jnp.where(
                        lower, grad_ref[rows, at].astype(jnp.float32), pltpu.roll(out, half, 1)
                    ).astype(jnp.bfloat16)
            return sums[0] + q_sum, sums[1] + k_sum

        zero = jnp.zeros((1, wide), jnp.float32)
        q_sum, k_sum = lax.fori_loop(0, blocks, finish, (zero, zero))
        gain_ref[0:1, :] += q_sum
        gain_ref[1:2, :] += k_sum


def attend(x, cq, ck, q_gain, k_gain, heads, half):
    slot = x.shape[0]
    wide = 2 * half
    pairs = heads // 2
    block = min(512, slot)
    constant = lambda rows: pl.BlockSpec((rows, wide), lambda j: (0, 0))
    area = slot * (slot + block) // 2
    return pl.pallas_call(
        functools.partial(attend_kernel, heads, half, block),
        grid=(pairs,),
        in_specs=[
            pl.BlockSpec((slot, 3 * wide), lambda j: (0, j)),
            constant(slot),
            constant(slot),
            constant(1),
            constant(1),
        ],
        out_specs=[
            pl.BlockSpec((slot, wide), lambda j: (0, j)),
            pl.BlockSpec((2, slot, wide), lambda j: (j, 0, 0)),
            pl.BlockSpec((2, slot, wide), lambda j: (j, 0, 0)),
        ],
        out_shape=[
            jax.ShapeDtypeStruct((slot, pairs * wide), jnp.float32),
            jax.ShapeDtypeStruct((heads, slot, wide), jnp.bfloat16),
            jax.ShapeDtypeStruct((heads, slot, wide), jnp.bfloat16),
        ],
        scratch_shapes=[pltpu.VMEM((slot, wide), jnp.bfloat16)] * 2,
        cost_estimate=pl.CostEstimate(
            flops=4 * heads * area * wide,
            transcendentals=heads * area,
            bytes_accessed=slot * pairs * wide * 24,
        ),
        name="attend",
    )(x, cq, ck, q_gain, k_gain)


def attend_back(x, qb, kf, att, grad, q_gain, k_gain, heads, half):
    slot = x.shape[0]
    wide = 2 * half
    pairs = heads // 2
    block = min(512, slot)
    area = slot * (slot + block) // 2
    gain = pl.BlockSpec((1, wide), lambda j: (0, 0))
    tall = pl.BlockSpec((2, slot, wide), lambda j: (j, 0, 0))
    column = pl.BlockSpec((slot, wide), lambda j: (0, j))
    return pl.pallas_call(
        functools.partial(attend_back_kernel, half, block),
        grid=(pairs,),
        in_specs=[
            pl.BlockSpec((slot, 3 * wide), lambda j: (0, j)),
            tall,
            tall,
            column,
            column,
            gain,
            gain,
        ],
        out_specs=[
            pl.BlockSpec((slot, 3 * wide), lambda j: (0, j)),
            pl.BlockSpec((slot, wide), lambda j: (0, 0)),
            pl.BlockSpec((8, wide), lambda j: (0, 0)),
        ],
        out_shape=[
            jax.ShapeDtypeStruct((slot, 3 * pairs * wide), jnp.bfloat16),
            jax.ShapeDtypeStruct((slot, wide), jnp.float32),
            jax.ShapeDtypeStruct((8, wide), jnp.float32),
        ],
        scratch_shapes=[
            pltpu.VMEM((slot, wide), jnp.bfloat16),
            pltpu.VMEM((slot, wide), jnp.bfloat16),
            pltpu.VMEM((wide, slot), jnp.bfloat16),
            pltpu.VMEM((wide, slot), jnp.float32),
            pltpu.VMEM((slot, wide), jnp.float32),
            pltpu.VMEM((slot, wide), jnp.float32),
        ],
        cost_estimate=pl.CostEstimate(
            flops=10 * heads * area * wide,
            transcendentals=heads * area,
            bytes_accessed=slot * pairs * wide * 40,
        ),
        name="attend_back",
    )(x, qb, kf, att, grad, q_gain, k_gain)


def split_pieces(values):
    high = lax.reduce_precision(values, 8, 7)
    middle = lax.reduce_precision(values - high, 8, 7)
    return high, middle, lax.reduce_precision(values - high - middle, 8, 7)


def bias_pieces(cumulative, length, slot, heads, wide):
    live = (jnp.arange(slot) < length)[:, None]
    last = lax.dynamic_slice_in_dim(cumulative, length - 1, 1, 0)
    query_side = jnp.where(live, cumulative, last)
    pad = jnp.zeros((slot, wide - 3 * heads), jnp.float32)
    high, middle, low = split_pieces(-cumulative)
    key_side = (jnp.where(live, high, NEGATIVE), jnp.where(live, middle, 0.0), jnp.where(live, low, 0.0))
    return (
        jnp.concatenate(split_pieces(query_side) + (pad,), axis=1).astype(jnp.bfloat16),
        jnp.concatenate(key_side + (pad,), axis=1).astype(jnp.bfloat16),
    )


def rms_scale(values):
    return lax.rsqrt(jnp.mean(values * values, axis=-1, keepdims=True) + EPSILON)


def norm_backward(values, scaling, grad_normed):
    cubed = scaling * scaling * scaling
    return scaling * grad_normed - values * cubed * jnp.mean(
        grad_normed * values, axis=-1, keepdims=True
    )


def gather(values, axis_name):
    return lax.all_gather(values, axis_name, axis=0, tiled=True)


def scatter(values, axis_name):
    return lax.psum_scatter(
        values.astype(jnp.bfloat16), axis_name, scatter_dimension=0, tiled=True
    ).astype(jnp.float32)


def pair_major(query, key, value, wide):
    pairs = query.shape[1] // wide
    return [
        part[:, j * wide : (j + 1) * wide] for j in range(pairs) for part in (query, key, value)
    ]


def from_pair_major(joined, wide):
    pairs = joined.shape[1] // (3 * wide)
    return [
        jnp.concatenate(
            [joined[:, (3 * j + i) * wide : (3 * j + i + 1) * wide] for j in range(pairs)], axis=1
        )
        for i in range(3)
    ]


def per_device(
    tokens,
    attn_gain,
    w_query,
    w_key,
    w_value,
    w_outgate,
    w_forget,
    forget_bias,
    w_output,
    query_gain,
    key_gain,
    mlp_gain,
    w_gate,
    w_up,
    w_down,
    lengths,
    out_grad,
):
    tensor_count = lax.axis_size("tensor")
    tensor_index = lax.axis_index("tensor")
    data_index = lax.axis_index("dp")
    local_rows = tokens.shape[0]
    slot = local_rows * tensor_count
    heads = w_forget.shape[1]
    half = query_gain.shape[0]
    wide = 2 * half
    width = heads * half
    hidden_width = w_gate.shape[1]
    shard = attn_gain.shape[0]
    length = lengths[0]

    small = jnp.concatenate(
        [
            w_forget,
            attn_gain[:, None],
            mlp_gain[:, None],
            jnp.zeros((shard, wide - heads - 2), jnp.bfloat16),
        ],
        axis=1,
    )
    first_full = gather(
        jnp.concatenate(pair_major(w_query, w_key, w_value, wide) + [small], axis=1), "dp"
    )
    second_full = gather(jnp.concatenate([w_outgate, w_output.T], axis=1), "dp")
    third_full = gather(jnp.concatenate([w_gate, w_up, w_down.T], axis=1), "dp")
    qkv_full = first_full[:, : 3 * width]
    small_full = first_full[:, 3 * width :]
    gain_one = small_full[:, heads].astype(jnp.float32)
    gain_two = small_full[:, heads + 1].astype(jnp.float32)
    outgate_full = second_full[:, :width]
    output_turned = second_full[:, width:]
    gate_full = third_full[:, :hidden_width]
    up_full = third_full[:, hidden_width : 2 * hidden_width]
    down_turned = third_full[:, 2 * hidden_width :]

    rows_float = tokens.astype(jnp.float32)
    scale_one = rms_scale(rows_float)
    normed_low = (rows_float * scale_one * gain_one).astype(jnp.bfloat16)
    normed_all = gather(normed_low, "tensor")
    projected = nn(normed_all, first_full)
    gate_logit = nn(normed_all, outgate_full)
    bias_local = lax.dynamic_slice_in_dim(forget_bias, tensor_index * heads, heads, 0)
    forget_logit = projected[:, 3 * width : 3 * width + heads] + bias_local[None, :]
    cumulative = jnp.cumsum(jax.nn.log_sigmoid(forget_logit), axis=0)
    query_pieces, key_pieces = bias_pieces(cumulative, length, slot, heads, wide)
    query_gain_wide = jnp.tile(query_gain.astype(jnp.float32), 2)[None]
    key_gain_wide = jnp.tile(key_gain.astype(jnp.float32), 2)[None]
    attended, query_feature, key_feature = attend(
        projected, query_pieces, key_pieces, query_gain_wide, key_gain_wide, heads, half
    )
    gate_open = jax.nn.sigmoid(gate_logit)
    gated_low = (attended * gate_open).astype(jnp.bfloat16)
    mixed = rows_float + scatter(nt(gated_low, output_turned), "tensor")

    scale_two = rms_scale(mixed)
    normed_mid = (mixed * scale_two * gain_two).astype(jnp.bfloat16)
    mid_all = gather(normed_mid, "tensor")
    gate_value = nn(mid_all, gate_full)
    up_value = nn(mid_all, up_full)
    gate_sigmoid = jax.nn.sigmoid(gate_value)
    gate_silu = gate_value * gate_sigmoid
    hidden_low = (gate_silu * up_value).astype(jnp.bfloat16)
    mixed_out = (mixed + scatter(nt(hidden_low, down_turned), "tensor")).astype(jnp.bfloat16)

    live_rows = tensor_index * local_rows + jnp.arange(local_rows) < length
    grad_out = jnp.where(live_rows[:, None], out_grad, jnp.zeros_like(out_grad))
    grad_out_all = gather(grad_out, "tensor")
    grad_hidden = nn(grad_out_all, down_turned)
    grad_down = tn(grad_out_all, hidden_low).astype(jnp.bfloat16)
    grad_gate_low = (
        grad_hidden * up_value * gate_sigmoid * (1.0 + gate_value * (1.0 - gate_sigmoid))
    ).astype(jnp.bfloat16)
    grad_up_low = (grad_hidden * gate_silu).astype(jnp.bfloat16)
    grad_mid = scatter(nt(grad_gate_low, gate_full) + nt(grad_up_low, up_full), "tensor")
    grad_gate_w = tn(mid_all, grad_gate_low).astype(jnp.bfloat16)
    grad_up_w = tn(mid_all, grad_up_low).astype(jnp.bfloat16)
    grad_gain_two = jnp.sum(grad_mid * mixed * scale_two, axis=0)
    grad_mixed = grad_out.astype(jnp.float32) + norm_backward(mixed, scale_two, grad_mid * gain_two)
    grad_mixed_all = gather(grad_mixed.astype(jnp.bfloat16), "tensor")
    grad_third = jnp.concatenate([grad_gate_w, grad_up_w, grad_down], axis=1)
    grad_third, grad_mixed_all = lax.optimization_barrier((grad_third, grad_mixed_all))
    third_sum = scatter(grad_third, "dp")

    grad_output_w = tn(grad_mixed_all, gated_low).astype(jnp.bfloat16)
    grad_gated = nn(grad_mixed_all, output_turned)
    grad_attended_low = (grad_gated * gate_open).astype(jnp.bfloat16)
    grad_gate_logit_low = (grad_gated * attended * gate_open * (1.0 - gate_open)).astype(
        jnp.bfloat16
    )
    grad_outgate_w = tn(normed_all, grad_gate_logit_low).astype(jnp.bfloat16)
    grad_qkv, grad_cumulative, gain_sums = attend_back(
        projected,
        query_feature,
        key_feature,
        attended,
        grad_attended_low,
        query_gain_wide,
        key_gain_wide,
        heads,
        half,
    )
    grad_log_forget = jnp.cumsum(grad_cumulative[::-1, :heads], axis=0)[::-1]
    grad_forget_low = (grad_log_forget * jax.nn.sigmoid(-forget_logit)).astype(jnp.bfloat16)
    grad_forget_wide = jnp.pad(grad_forget_low, ((0, 0), (0, wide - heads)))
    grad_bias_local = jnp.sum(grad_forget_low.astype(jnp.float32), axis=0)
    grad_normed = scatter(
        nt(grad_qkv, qkv_full)
        + nt(grad_gate_logit_low, outgate_full)
        + nt(grad_forget_wide, small_full),
        "tensor",
    )
    grad_first = jnp.concatenate(
        [
            tn(normed_all, grad_qkv).astype(jnp.bfloat16),
            tn(normed_all, grad_forget_wide).astype(jnp.bfloat16),
            grad_outgate_w,
            grad_output_w,
        ],
        axis=1,
    )
    first_sum = scatter(grad_first, "dp")
    grad_gain_one = jnp.sum(grad_normed * rows_float * scale_one, axis=0)
    tokens_grad = grad_mixed + norm_backward(rows_float, scale_one, grad_normed * gain_one)
    bias_spread = lax.dynamic_update_slice_in_dim(
        jnp.zeros(forget_bias.shape, jnp.float32), grad_bias_local, tensor_index * heads, 0
    )
    gain_one_sum, gain_two_sum, query_sum, key_sum, bias_sum = lax.psum(
        (grad_gain_one, grad_gain_two, gain_sums[0, :half], gain_sums[1, :half], bias_spread),
        ("dp", "tensor"),
    )
    own = data_index * shard
    grad_query_w, grad_key_w, grad_value_w = from_pair_major(first_sum[:, : 3 * width], wide)
    after = 3 * width + wide
    return (
        mixed_out,
        tokens_grad,
        lax.dynamic_slice_in_dim(gain_one_sum, own, shard, 0),
        grad_query_w,
        grad_key_w,
        grad_value_w,
        first_sum[:, after : after + width],
        first_sum[:, 3 * width : 3 * width + heads],
        bias_sum,
        first_sum[:, after + width :].T,
        query_sum,
        key_sum,
        lax.dynamic_slice_in_dim(gain_two_sum, own, shard, 0),
        third_sum[:, :hidden_width],
        third_sum[:, hidden_width : 2 * hidden_width],
        third_sum[:, 2 * hidden_width :].T,
    )


def solution(mesh):
    in_specs = (
        P(("dp", "tensor"), None),
        P("dp"),
        P("dp", "tensor"),
        P("dp", "tensor"),
        P("dp", "tensor"),
        P("dp", "tensor"),
        P("dp", "tensor"),
        P(),
        P("tensor", "dp"),
        P(),
        P(),
        P("dp"),
        P("dp", "tensor"),
        P("dp", "tensor"),
        P("tensor", "dp"),
        P("dp"),
        P(("dp", "tensor"), None),
    )
    out_specs = (
        P(("dp", "tensor"), None),
        P(("dp", "tensor"), None),
        P("dp"),
        P("dp", "tensor"),
        P("dp", "tensor"),
        P("dp", "tensor"),
        P("dp", "tensor"),
        P("dp", "tensor"),
        P(),
        P("tensor", "dp"),
        P(),
        P(),
        P("dp"),
        P("dp", "tensor"),
        P("dp", "tensor"),
        P("tensor", "dp"),
    )
    return jax.shard_map(
        per_device, mesh=mesh, in_specs=in_specs, out_specs=out_specs, check_vma=False
    )
```

time: 2020 us -> 1220 us (0.60)
  matrix products: 587 us -> 193 us
  waiting for transfers between devices: 956 us -> 743 us
  other arithmetic: 204 us -> 48 us
  Pallas kernels: 0 us -> 107 us
  local copies, waits for them, and re-layouts: 127 us -> 66.2 us
  blocking collectives: 94.3 us -> 40.5 us
    reduce_scatter x12 -> x4, waiting for transfers between devices: 580 us -> 180 us  [scatter(): lax.psum_scatter(values.astype(jnp.bfloat16), axis_name, scatter_dimensio...]
    dot_general x55 -> x20, matrix products: 587 us -> 193 us  [the longest x7 71.7 us: nt(): lax.dot_general(left, right, (((1,), (1,)), ((), ())), preferred_element_...]
    unnamed x26 -> x15, waiting for transfers between devices: 5.17 us -> 217 us
    reduce_sum x11 -> x0, other arithmetic: 131 us -> none  [the longest x4 66.4 us: back_block(): grad_cum_rows = jnp.transpose(jnp.sum(scores_float, axis=2))]
    pallas_call x0 -> x2, Pallas kernels: none -> 107 us  [the longest x1 72.2 us: attend_back(): pl.pallas_call(functools.partial(attend_back_kernel, half, block), grid=(...]
    dynamic_update_slice x12 -> x0, local copies, waits for them, and re-layouts: 67.5 us -> none  [attend_slot(): attended, log_total = lax.map(forward_block, starts)]
    all_gather x1 -> x0, blocking collectives: 30.6 us -> none  [per_device(): lax.all_gather(w_forget, 'dp', axis=0, tiled=True)]
    unnamed x129 -> x119, local copies, waits for them, and re-layouts: 18 us -> 44.5 us
  transfers between devices with their start and end apart: 25 -> 13, of which waited for: 19 -> 12; matrix products, arithmetic and copies ran while one was open for 41% -> 13% of each run, Pallas kernels for 0% -> 3%
where the time goes in v1:
time: 1220 us; the launch traced here: 1210 us
  waiting for transfers between devices  743 us (61%)
  matrix products  193 us (16%)
  Pallas kernels  107 us (9%)
  local copies, waits for them, and re-layouts  66.2 us (5%)
  other arithmetic  48 us (4%)
  blocking collectives  40.5 us (3%)
  between operations  15.6 us (1%)
    all_gather x7, waiting for transfers between devices, gather(): return lax.all_gather(values, axis_name, axis=0, tiled=True)  346 us
    unnamed x15, waiting for transfers between devices  217 us
    reduce_scatter x4, waiting for transfers between devices, scatter(): lax.psum_scatter(values.astype(jnp.bfloat16), axis_name, scatter_dimensio...  180 us
    pallas_call x1, Pallas kernels, attend_back(): pl.pallas_call(functools.partial(attend_back_kernel, half, block), grid=(...  72.2 us
    dot_general x7, matrix products, nt(): lax.dot_general(left, right, (((1,), (1,)), ((), ())), preferred_element_...  71.7 us
    dot_general x6, matrix products, nn(): return jnp.dot(left, right, preferred_element_type=jnp.float32)  68.2 us
    dot_general x7, matrix products, tn(): lax.dot_general(left, right, (((0,), (0,)), ((), ())), preferred_element_...  53.4 us
    unnamed x119, local copies, waits for them, and re-layouts  44.5 us
  transfers between devices with their start and end apart: 13, of which 12 were waited for; matrix products, arithmetic and copies ran while one was open for 13% of the time, Pallas kernels for 3%

profile of v1, /device:TPU:0, one launch (start us, length us, event | category | flops | bytes accessed | tf_op | source)
XLA Modules:
  0.0 1213.7 jit_solution(16862332393349118707)
XLA Ops:
  13.6 71.3 %all-gather.8.cloned.1.call-done = bf16[1536,1280]{1,0:T(8,128)(2,1)} async-done(((bf16[192,1280]{1,0:T(8,128)(2,1)}), bf16[1536,1280]{1,0:T(8,128)(2,1)}) %all-gather.8.cloned.1.call-update) | async-done | bytes 3932176 | tf_op jit(solution)/shard_map/all_gather | solution.py:365
  84.9 1.7 convert_reduce_fusion.1
  86.6 1.6 fusion.15
  91.1 42.2 %all-gather.10.cloned.1.call-done = bf16[2048,1536]{1,0:T(8,128)(2,1)} async-done(((bf16[512,1536]{1,0:T(8,128)(2,1)}), bf16[2048,1536]{1,0:T(8,128)(2,1)}) %all-gather.10.cloned.1.call-update) | async-done | bytes 6291472 | tf_op jit(solution)/shard_map/all_gather | solution.py:365
  133.3 11.5 fusion.55.x_ref
  144.9 4.0 copy-done.11
  149.9 1.7 reduce-window.14
  152.4 1.4 fusion.32
  153.8 2.0 maximum_maximum_fusion.1
  155.8 34.4 %attend.1 = (f32[2048,384]{1,0:T(8,128)}, bf16[6,2048,128]{2,1,0:T(8,128)(2,1)}, bf16[6,2048,128]{2,1,0:T(8,128)(2,1)}) custom-call(f32[2048,1280]{1,0:T(8,128)} %copy-done.11, bf16[2048,128]{1,0:T(8,128)(2,1)} %get-tuple-element.152.cq_ref, bf16[2048,128]{1,0:T(8,128)(2,1)} %get-tuple-element.151.ck_ref, f32[1,128]{1,0:T(1,128)} %broadcast_in_dim_tile.6.qg_ref, ...), custom_call_target="tpu_custom_call" | custom-call | flops 8053063680 | bytes 18874368 | tf_op jit(solution)/shard_map/attend/pallas_call | solution.py:256
  190.2 9.5 multiply_convert_fusion.6
  200.9 5.4 convolution_convert_fusion.2
  206.4 1.3 copy-done.4
  207.7 1.3 broadcast_select_fusion
  209.1 2.3 pad_maximum_fusion.2
  211.4 53.9 %reduce-scatter.11.cloned.1.call-done = bf16[512,1536]{1,0:T(8,128)(2,1)} async-done(((bf16[2048,1536]{1,0:T(8,128)(2,1)}), bf16[512,1536]{1,0:T(8,128)(2,1)}) %reduce-scatter.11.cloned.1.call-update) | async-done | bytes 1572880 | tf_op jit(solution)/shard_map/reduce_scatter | solution.py:369
  265.3 2.1 multiply_reduce_fusion
  267.5 1.7 multiply_convert_fusion.5
  269.3 44.4 %all-gather.18.cloned.1.call-done = bf16[2048,1536]{1,0:T(8,128)(2,1)} async-done(((bf16[512,1536]{1,0:T(8,128)(2,1)}), bf16[2048,1536]{1,0:T(8,128)(2,1)}) %all-gather.18.cloned.1.call-update) | async-done | bytes 6291472 | tf_op jit(solution)/shard_map/all_gather | solution.py:365
  313.7 139.3 %all-gather.16.cloned.1.call-done = bf16[1536,3072]{1,0:T(8,128)(2,1)} async-done(((bf16[192,3072]{1,0:T(8,128)(2,1)}), bf16[1536,3072]{1,0:T(8,128)(2,1)}) %all-gather.16.cloned.1.call-update) | async-done | bytes 9437200 | tf_op jit(solution)/shard_map/all_gather | solution.py:365
  453.0 12.6 %fusion.20 = f32[2048,1024]{1,0:T(8,128)} fusion(bf16[2048,1536]{1,0:T(8,128)(2,1)} %all-gather.18.cloned.1.call-done, bf16[1536,3072]{1,0:T(8,128)(2,1)} %all-gather.16.cloned.1.call-done), kind=kOutput, calls=%fused_computation.53 | convolution fusion | flops 6442450944 | bytes 17825792 | tf_op jit(solution)/shard_map/dot_general | solution.py:28
  465.6 33.6 %all-gather.14.cloned.1.call-done = bf16[2048,1536]{1,0:T(8,128)(2,1)} async-done(((bf16[512,1536]{1,0:T(8,128)(2,1)}), bf16[2048,1536]{1,0:T(8,128)(2,1)}) %all-gather.14.cloned.1.call-update) | async-done | bytes 6291472 | tf_op jit(solution)/shard_map/all_gather | solution.py:365
  499.1 12.4 %fusion.24 = f32[2048,1024]{1,0:T(8,128)} fusion(bf16[2048,1536]{1,0:T(8,128)(2,1)} %all-gather.14.cloned.1.call-done, bf16[1536,3072]{1,0:T(8,128)(2,1)} %all-gather.16.cloned.1.call-done), kind=kOutput, calls=%fused_computation.57 | convolution fusion | flops 6442450944 | bytes 17825792 | tf_op jit(solution)/shard_map/dot_general | solution.py:28
  511.5 17.3 %multiply_convert_fusion.1 = (bf16[2048,1024]{1,0:T(8,128)(2,1)}, bf16[2048,1024]{1,0:T(8,128)(2,1)}, bf16[2048,1024]{1,0:T(8,128)(2,1)}) fusion(f32[2048,1024]{1,0:T(8,128)} %fusion.20, f32[2048,1024]{1,0:T(8,128)} %fusion.24, bf16[2048,1536]{1,0:T(8,128)(2,1)S(1)} %copy-done.38, bf16[1536,3072]{1,0:T(8,128)(2,1)} %all-gather.16.cloned.1.call-done), kind=kOutput, calls=%fused_computation.4 | convolution fusion | flops 6473908224 | bytes 38797312 | tf_op jit(solution)/shard_map/dot_general | solution.py:28
  528.8 9.5 fusion.26
  538.3 11.8 add_convert_fusion.1
  550.2 58.9 %reduce-scatter.15.cloned.1.call-done = bf16[512,1536]{1,0:T(8,128)(2,1)} async-done(((bf16[2048,1536]{1,0:T(8,128)(2,1)}), bf16[512,1536]{1,0:T(8,128)(2,1)}) %reduce-scatter.15.cloned.1.call-update) | async-done | bytes 1572880 | tf_op jit(solution)/shard_map/reduce_scatter | solution.py:369
  609.2 3.3 fusion.12
  612.6 2.4 fusion.49
  615.1 10.3 convolution_convert_fusion.4
  625.4 9.4 convolution_convert_fusion.5
  634.9 7.3 convolution_convert_fusion.3
  642.2 4.4 pad_maximum_fusion
  646.6 15.0 %all-gather.20.cloned.1.call-done = bf16[2048,1536]{1,0:T(8,128)(2,1)} async-done(((bf16[512,1536]{1,0:T(8,128)(2,1)}), bf16[2048,1536]{1,0:T(8,128)(2,1)}) %all-gather.20.cloned.1.call-update) | async-done | bytes 6291472 | tf_op jit(solution)/shard_map/all_gather | solution.py:365
  661.6 6.6 convolution_convert_fusion.6
  669.1 4.8 multiply_convert_fusion.3
  673.9 72.2 %attend_back.1 = (bf16[2048,1152]{1,0:T(8,128)(2,1)}, f32[2048,128]{1,0:T(8,128)}, f32[8,128]{1,0:T(8,128)}) custom-call(f32[2048,1280]{1,0:T(8,128)} %copy-done.11, bf16[6,2048,128]{2,1,0:T(8,128)(2,1)} %get-tuple-element.25.qb_ref, bf16[6,2048,128]{2,1,0:T(8,128)(2,1)} %get-tuple-element.26.kf_ref, f32[2048,384]{1,0:T(8,128)} %get-tuple-element.24.att_ref, ...), custom_call_target="tpu_custom_call" | custom-call | flops 20132659200 | bytes 31457280 | tf_op jit(solution)/shard_map/attend_back/pallas_call | solution.py:295
  746.1 6.8 rev.6
  753.3 1.7 reduce-window.16
  756.2 1.7 convert_reduce_fusion
  757.9 5.9 convolution_convert_fusion.7
  763.8 3.8 convolution_convert_fusion.8
  767.7 10.0 convolution_convert_fusion
  777.8 3.1 pad_maximum_fusion.1
  780.8 8.7 copy.105
  789.6 1.3 copy-done.7
  790.9 8.2 fusion.41
  799.2 12.9 %fusion.4 = f32[2048,1536]{1,0:T(8,128)} fusion(bf16[2048,1152]{1,0:T(8,128)(2,1)} %get-tuple-element.28, bf16[1536,1280]{1,0:T(8,128)(2,1)S(1)} %copy-done.13), kind=kOutput, calls=%fused_computation.27 | convolution fusion | flops 7247757312 | bytes 20840448 | tf_op jit(solution)/shard_map/dot_general | solution.py:16
  812.0 12.3 %add_convert_fusion = bf16[2048,1536]{1,0:T(8,128)(2,1)} fusion(f32[2048,1536]{1,0:T(8,128)} %fusion.4, f32[2048,1536]{1,0:T(8,128)} %fusion.41, bf16[2048,6]{1,0:T(8,128)(2,1)S(1)} %get-tuple-element.108, bf16[1536,1280]{1,0:T(8,128)(2,1)S(1)} %copy-done.13), kind=kOutput, calls=%fused_computation | convolution fusion | flops 814743552 | bytes 32374784 | tf_op jit(solution)/shard_map/dot_general | solution.py:16
  824.4 11.6 convolution_convert_fusion.1
  836.1 12.6 %copy.107 = bf16[1536,3072]{1,0:T(8,128)(2,1)} copy(bf16[1536,3072]{0,1:T(8,128)(2,1)} %pad_maximum_fusion) | data formatting | bytes 18874368
  850.3 57.5 %reduce-scatter.19.cloned.1.call-done = bf16[192,2048]{1,0:T(8,128)(2,1)} async-done(((bf16[1536,2048]{1,0:T(8,128)(2,1)}), bf16[192,2048]{1,0:T(8,128)(2,1)}) %reduce-scatter.19.cloned.1.call-update) | async-done | bytes 786448
  907.7 1.4 copy.106
  909.8 1.5 convert_element_type.157
  914.0 2.1 copy.98
  918.9 49.5 %reduce-scatter.17.cloned.1.call-done = bf16[512,1536]{1,0:T(8,128)(2,1)} async-done(((bf16[2048,1536]{1,0:T(8,128)(2,1)}), bf16[512,1536]{1,0:T(8,128)(2,1)}) %reduce-scatter.17.cloned.1.call-update) | async-done | bytes 1572880 | tf_op jit(solution)/shard_map/reduce_scatter | solution.py:369
  968.4 2.6 fusion.19
  971.1 40.5 %all-reduce.1 = (f32[1536]{0:T(1024)S(1)}, f32[24]{0:T(128)}, f32[64]{0:T(128)}, f32[64]{0:T(128)}, f32[1536]{0:T(1024)S(1)}) all-reduce(f32[1536]{0:T(1024)S(1)} %get-tuple-element.100, f32[24]{0:T(128)S(1)} %copy-done.37, f32[64]{0:T(128)S(1)} %copy-done.35, ...), channel_id=1, replica_groups=mesh['dp'=8,'tensor'=4] {'dp','tensor'}, use_global_device_ids=true, to_apply=%region_13.14 | all-reduce | flops 3224 | bytes 25792 | tf_op jit(solution)/shard_map/psum | solution.py:538
  1012.8 17.5 %reduce-scatter.13.cloned.1.call-done = bf16[512,1536]{1,0:T(8,128)(2,1)} async-done(((bf16[2048,1536]{1,0:T(8,128)(2,1)}), bf16[512,1536]{1,0:T(8,128)(2,1)}) %reduce-scatter.13.cloned.1.call-update) | async-done | bytes 1572880 | tf_op jit(solution)/shard_map/reduce_scatter | solution.py:369
  1030.4 6.0 fusion.7
  1036.4 159.7 %reduce-scatter.21.cloned.1.call-done = bf16[192,3072]{1,0:T(8,128)(2,1)} async-done(((bf16[1536,3072]{1,0:T(8,128)(2,1)}), bf16[192,3072]{1,0:T(8,128)(2,1)}) %reduce-scatter.21.cloned.1.call-update) | async-done | bytes 1179664
  1196.1 1.6 copy.108
  1198.9 1.9 convert_element_type.159
  1200.8 2.4 copy.101
  (187 shorter events, 28.2 us)
Async XLA Ops:
  7.2 5.4 copy-start
  7.2 77.7 %all-gather.8.cloned.1.call-start = ((), (), s32[]{:S(2)}) async-start(), calls=%async_computation.6 | async-start | bytes 4423680 | tf_op jit(solution)/shard_map/all_gather | solution.py:365
  12.5 120.8 %all-gather.10.cloned.1.call-start = ((), (), s32[]{:S(2)}) async-start(), calls=%async_computation.7 | async-start | bytes 7864320 | tf_op jit(solution)/shard_map/all_gather | solution.py:365
  13.0 75.3 %copy-start.16 = (bf16[384,192]{0,1:T(8,128)(2,1)S(1)}, bf16[384,192]{0,1:T(8,128)(2,1)}, u32[]{:S(2)}) copy-start(bf16[384,192]{0,1:T(8,128)(2,1)} %param.25) | copy-start | bytes 442372
  13.0 75.3 %copy-start.17 = (bf16[192,384]{1,0:T(8,128)(2,1)S(1)}, bf16[192,384]{1,0:T(8,128)(2,1)}, u32[]{:S(2)}) copy-start(bf16[192,384]{1,0:T(8,128)(2,1)} %param.22) | copy-start | bytes 442372
  13.6 75.4 %copy-start.23 = (f32[512]{0:T(512)}, f32[512]{0:T(512)S(1)}, u32[]{:S(2)}) copy-start(f32[512]{0:T(512)S(1)} %get-tuple-element.148) | copy-start | bytes 6148
  13.6 76.2 %copy-start.40 = (bf16[64]{0:T(256)(128)(2,1)S(1)}, bf16[64]{0:T(256)(128)(2,1)}, u32[]{:S(2)}) copy-start(bf16[64]{0:T(256)(128)(2,1)} %param.26) | copy-start | bytes 388
  13.6 76.8 %copy-start.41 = (bf16[64]{0:T(256)(128)(2,1)S(1)}, bf16[64]{0:T(256)(128)(2,1)}, u32[]{:S(2)}) copy-start(bf16[64]{0:T(256)(128)(2,1)} %param.27) | copy-start | bytes 388
  13.6 77.4 %copy-start.42 = (f32[24]{0:T(128)S(1)}, f32[24]{0:T(128)}, u32[]{:S(2)}) copy-start(f32[24]{0:T(128)} %param.24) | copy-start | bytes 292
  86.6 46.8 %copy-start.18 = (f32[1536]{0:T(1024)}, f32[1536]{0:T(1024)S(1)}, u32[]{:S(2)}) copy-start(f32[1536]{0:T(1024)S(1)} %get-tuple-element.99) | copy-start | bytes 18436
  86.6 525.9 %copy-start.14 = (f32[1536]{0:T(1024)}, f32[1536]{0:T(1024)S(1)}, u32[]{:S(2)}) copy-start(f32[1536]{0:T(1024)S(1)} %get-tuple-element.98) | copy-start | bytes 18436
  88.2 102.0 %all-gather.12.cloned.1.call-start = ((), (), s32[]{:S(2)}) async-start(), calls=%async_computation.8 | async-start | bytes 2654208 | tf_op jit(solution)/shard_map/all_gather | solution.py:365
  89.0 176.3 %reduce-scatter.11.cloned.1.call-start = ((), (), s32[]{:S(2)}) async-start(), calls=%async_computation.9 | async-start | bytes 7864320 | tf_op jit(solution)/shard_map/reduce_scatter | solution.py:369
  91.0 53.8 %copy-start.32 = (f32[6]{0:T(128)}, f32[6]{0:T(128)S(1)}, u32[]{:S(2)}) copy-start(f32[6]{0:T(128)S(1)} %dynamic_slice.10) | copy-start | bytes 76
  144.9 4.0 copy-start.11
  190.2 10.7 copy-start.9
  206.3 1.4 copy-start.4
  206.3 2.8 copy-start.12
  206.3 107.4 %all-gather.18.cloned.1.call-start = ((), (), s32[]{:S(2)}) async-start(), calls=%async_computation.13 | async-start | bytes 7864320 | tf_op jit(solution)/shard_map/all_gather | solution.py:365
  207.7 404.8 %copy-start.30 = (pred[512]{0:T(512)(128)(4,1)}, pred[512]{0:T(512)(128)(4,1)S(1)}, u32[]{:S(2)}) copy-start(pred[512]{0:T(512)(128)(4,1)S(1)} %add_compare_fusion) | copy-start | bytes 1540
  209.0 244.0 %all-gather.16.cloned.1.call-start = ((), (), s32[]{:S(2)}) async-start(), calls=%async_computation.11 | async-start | bytes 10616832 | tf_op jit(solution)/shard_map/all_gather | solution.py:365
  211.4 287.7 %all-gather.14.cloned.1.call-start = ((), (), s32[]{:S(2)}) async-start(), calls=%async_computation.10 | async-start | bytes 7864320 | tf_op jit(solution)/shard_map/all_gather | solution.py:365
  265.3 2.1 copy-start.2
  267.4 345.1 %copy-start.20 = (f32[512]{0:T(512)}, f32[512]{0:T(512)S(1)}, u32[]{:S(2)}) copy-start(f32[512]{0:T(512)S(1)} %get-tuple-element.150) | copy-start | bytes 6148
  267.4 345.1 %copy-start.25 = (f32[512]{0:T(512)}, f32[512]{0:T(512)S(1)}, u32[]{:S(2)}) copy-start(f32[512]{0:T(512)S(1)} %get-tuple-element.149) | copy-start | bytes 6148
  269.2 339.9 %reduce-scatter.15.cloned.1.call-start = ((), (), s32[]{:S(2)}) async-start(), calls=%async_computation.14 | async-start | bytes 7864320 | tf_op jit(solution)/shard_map/reduce_scatter | solution.py:369
  499.1 12.4 %copy-start.38 = (bf16[2048,1536]{1,0:T(8,128)(2,1)S(1)}, bf16[2048,1536]{1,0:T(8,128)(2,1)}, u32[]{:S(2)}) copy-start(bf16[2048,1536]{1,0:T(8,128)(2,1)} %all-gather.14.cloned.1.call-done) | copy-start | bytes 18874372
  550.2 111.4 %all-gather.20.cloned.1.call-start = ((), (), s32[]{:S(2)}) async-start(), calls=%async_computation.15 | async-start | bytes 7864320 | tf_op jit(solution)/shard_map/all_gather | solution.py:365
  609.2 3.4 copy-start.5
  609.2 3.4 copy-start.6
  612.5 2.5 copy-start.27
  615.0 292.7 %reduce-scatter.19.cloned.1.call-start = ((), (), s32[]{:S(2)}) async-start(), calls=%async_computation.17 | async-start | bytes 7077888
  615.1 10.3 copy-start.47
  615.1 19.8 %slice-start = ((s8[6291456]{0:T(1024)(128)(4,1)}), s8[4194304]{0:T(1024)(128)(4,1)S(1)}, s32[]{:S(2)}) async-start(s8[6291456]{0:T(1024)(128)(4,1)} %bitcast.87), calls=%async_computation.19 | async-start | bytes 8388608
  625.4 9.5 slice-start.1
  625.4 9.5 copy-start.48
  642.2 19.3 %copy-start.46 = (bf16[2048,384]{1,0:T(8,128)(2,1)S(1)}, bf16[2048,384]{1,0:T(8,128)(2,1)}, u32[]{:S(2)}) copy-start(bf16[2048,384]{1,0:T(8,128)(2,1)} %copy-done.45) | copy-start | bytes 4718596
  661.5 6.7 copy-start.10
  661.5 6.7 copy-start.39
  661.5 6.7 copy-start.43
  661.5 7.5 copy-start.44
  746.1 10.1 copy-start.33
  756.2 11.5 slice-start.2
  757.9 9.8 slice-start.3
  767.7 10.0 copy-start.8
  789.5 1.4 copy-start.7
  789.6 178.9 %reduce-scatter.17.cloned.1.call-start = ((), (), s32[]{:S(2)}) async-start(), calls=%async_computation.16 | async-start | bytes 7864320 | tf_op jit(solution)/shard_map/reduce_scatter | solution.py:369
  790.9 8.2 copy-start.13
  824.4 206.0 %reduce-scatter.13.cloned.1.call-start = ((), (), s32[]{:S(2)}) async-start(), calls=%async_computation.12 | async-start | bytes 7864320 | tf_op jit(solution)/shard_map/reduce_scatter | solution.py:369
  836.0 360.1 %reduce-scatter.21.cloned.1.call-start = ((), (), s32[]{:S(2)}) async-start(), calls=%async_computation.18 | async-start | bytes 10616832
  911.4 57.0 %copy-start.1 = (bf16[512,1536]{1,0:T(8,128)(2,1)S(1)}, bf16[512,1536]{1,0:T(8,128)(2,1)}, u32[]{:S(2)}) copy-start(bf16[512,1536]{1,0:T(8,128)(2,1)} %param.17) | copy-start | bytes 4718596
  911.4 57.0 %copy-start.19 = (f32[1536]{0:T(1024)S(1)}, f32[1536]{0:T(1024)}, u32[]{:S(2)}) copy-start(f32[1536]{0:T(1024)} %copy-done.18) | copy-start | bytes 18436
  914.0 116.4 %copy-start.3 = (bf16[512,1536]{1,0:T(8,128)(2,1)S(1)}, bf16[512,1536]{1,0:T(8,128)(2,1)}, u32[]{:S(2)}) copy-start(bf16[512,1536]{1,0:T(8,128)(2,1)} %reduce-scatter.11.cloned.1.call-done) | copy-start | bytes 4718596
  914.0 116.4 %copy-start.15 = (f32[1536]{0:T(1024)S(1)}, f32[1536]{0:T(1024)}, u32[]{:S(2)}) copy-start(f32[1536]{0:T(1024)} %copy-done.14) | copy-start | bytes 18436
  918.8 52.2 %copy-start.22 = (f32[1536]{0:T(1024)S(1)}, f32[1536]{0:T(1024)}, u32[]{:S(2)}) copy-start(f32[1536]{0:T(1024)} %get-tuple-element.96) | copy-start | bytes 18436
  918.8 52.2 %copy-start.34 = (f32[64]{0:T(128)S(1)}, f32[64]{0:T(128)}, u32[]{:S(2)}) copy-start(f32[64]{0:T(128)} %get-tuple-element.145) | copy-start | bytes 772
  918.8 52.2 %copy-start.35 = (f32[64]{0:T(128)S(1)}, f32[64]{0:T(128)}, u32[]{:S(2)}) copy-start(f32[64]{0:T(128)} %get-tuple-element.146) | copy-start | bytes 772
  918.8 52.2 %copy-start.37 = (f32[24]{0:T(128)S(1)}, f32[24]{0:T(128)}, u32[]{:S(2)}) copy-start(f32[24]{0:T(128)} %copy-done.36) | copy-start | bytes 292
  918.9 111.5 %copy-start.21 = (f32[512]{0:T(512)S(1)}, f32[512]{0:T(512)}, u32[]{:S(2)}) copy-start(f32[512]{0:T(512)} %copy-done.20) | copy-start | bytes 6148
  918.9 111.5 %copy-start.24 = (f32[512]{0:T(512)S(1)}, f32[512]{0:T(512)}, u32[]{:S(2)}) copy-start(f32[512]{0:T(512)} %copy-done.23) | copy-start | bytes 6148
  918.9 111.5 %copy-start.26 = (f32[512]{0:T(512)S(1)}, f32[512]{0:T(512)}, u32[]{:S(2)}) copy-start(f32[512]{0:T(512)} %copy-done.25) | copy-start | bytes 6148
  918.9 111.5 %copy-start.28 = (f32[512]{0:T(512)S(1)}, f32[512]{0:T(512)}, u32[]{:S(2)}) copy-start(f32[512]{0:T(512)} %copy-done.27) | copy-start | bytes 6148
  918.9 111.5 %copy-start.29 = (f32[512]{0:T(512)S(1)}, f32[512]{0:T(512)}, u32[]{:S(2)}) copy-start(f32[512]{0:T(512)} %get-tuple-element.147) | copy-start | bytes 6148
  918.9 111.5 %copy-start.31 = (pred[512]{0:T(512)(128)(4,1)S(1)}, pred[512]{0:T(512)(128)(4,1)}, u32[]{:S(2)}) copy-start(pred[512]{0:T(512)(128)(4,1)} %copy-done.30) | copy-start | bytes 1540
  (2 other events, 2.5 us)
Sparse Core Ops, SparseCore 0:
  12.6 72.1 all-gather.7
  88.3 44.9 all-gather.9
  136.1 51.7 all-gather.11
  206.4 58.8 reduce-scatter.10
  267.3 46.3 all-gather.17
  315.7 137.2 all-gather.15
  454.6 44.5 all-gather.13
  550.3 58.8 reduce-scatter.14
  615.1 46.3 all-gather.19
  789.7 117.9 reduce-scatter.18
  910.3 58.1 reduce-scatter.16
  970.8 59.5 reduce-scatter.12
  1034.0 162.1 reduce-scatter.20

commit v2 on v1

--- a/solution.py
+++ b/solution.py
@@ -329,6 +329,226 @@
         ),
         name="attend_back",
     )(x, qb, kf, att, grad, q_gain, k_gain)
+
+
+def tensor_peers():
+    me = lax.axis_index("tensor")
+    partner = me + 1 - 2 * lax.rem(me, 2)
+    across = lax.rem(me + 2, 4)
+    return me, partner, across, lax.rem(partner + 2, 4)
+
+
+def greet(names):
+    barrier = pltpu.get_barrier_semaphore()
+    for name in names:
+        pl.semaphore_signal(barrier, inc=1, device_id=name, device_id_type=pl.DeviceIdType.MESH)
+    pl.semaphore_wait(barrier, len(names))
+
+
+def send(source, target, sent, received, name):
+    return pltpu.make_async_remote_copy(
+        src_ref=source,
+        dst_ref=target,
+        send_sem=sent,
+        recv_sem=received,
+        device_id=name,
+        device_id_type=pl.DeviceIdType.MESH,
+    )
+
+
+def gather_kernel(count, chunks, *refs):
+    ins, outs = refs[:count], refs[count : 2 * count]
+    kept, near_out, near_in, far_out, far_in, pass_out, pass_in = refs[2 * count :]
+    me, partner, across, _ = tensor_peers()
+    greet(({"tensor": partner}, {"tensor": across}))
+    rows = ins[0].shape[0]
+    step = rows // chunks
+
+    def place(owner, c):
+        return pl.ds(pl.multiple_of(owner * rows + c * step, step), step)
+
+    own = pl.ds(pl.multiple_of(me * rows, rows), rows)
+    far, near, local, passed = [], [], [], []
+    for i in range(count):
+        for c in range(chunks):
+            far.append(
+                send(
+                    ins[i].at[pl.ds(c * step, step)],
+                    outs[i].at[place(me, c)],
+                    far_out.at[i, c],
+                    far_in.at[i, c],
+                    {"tensor": across},
+                )
+            )
+            far[-1].start()
+    for i in range(count):
+        near.append(
+            send(ins[i], outs[i].at[own], near_out.at[i], near_in.at[i], {"tensor": partner})
+        )
+        near[-1].start()
+        local.append(pltpu.make_async_copy(ins[i], outs[i].at[own], kept.at[i]))
+        local[-1].start()
+    for i in range(count):
+        for c in range(chunks):
+            far[i * chunks + c].wait_recv()
+            passed.append(
+                send(
+                    outs[i].at[place(across, c)],
+                    outs[i].at[place(across, c)],
+                    pass_out.at[i, c],
+                    pass_in.at[i, c],
+                    {"tensor": partner},
+                )
+            )
+            passed[-1].start()
+    for copy in local + near + passed:
+        copy.wait()
+    for copy in far:
+        copy.wait_send()
+
+
+def tensor_gather(arrays, number):
+    count, chunks = len(arrays), 4
+    rows, columns = arrays[0].shape
+    moved = count * rows * columns * 2
+    return pl.pallas_call(
+        functools.partial(gather_kernel, count, chunks),
+        in_specs=[pl.BlockSpec(memory_space=pltpu.VMEM)] * count,
+        out_specs=[pl.BlockSpec(memory_space=pl.ANY)] * count,
+        out_shape=[jax.ShapeDtypeStruct((4 * rows, columns), a.dtype) for a in arrays],
+        scratch_shapes=[
+            pltpu.SemaphoreType.DMA((count,)),
+            pltpu.SemaphoreType.DMA((count,)),
+            pltpu.SemaphoreType.DMA((count,)),
+        ]
+        + [pltpu.SemaphoreType.DMA((count, chunks))] * 4,
+        compiler_params=pltpu.CompilerParams(collective_id=number, has_side_effects=True),
+        cost_estimate=pl.CostEstimate(flops=0, transcendentals=0, bytes_accessed=80 * moved),
+        name="tensor_gather",
+    )(*arrays)
+
+
+def scatter_kernel(
+    chunks, p_ref, o_ref, given, own_in, outgoing, arriving, near_out, near_in, own_out, own_sem, far_out, far_in
+):
+    me, partner, across, opposite = tensor_peers()
+    greet(({"tensor": partner}, {"tensor": across}))
+    rows = o_ref.shape[0]
+    step = rows // chunks
+
+    def place(owner, c):
+        return pl.ds(pl.multiple_of(owner * rows + c * step, step), step)
+
+    near, far = [], []
+    for c in range(chunks):
+        near.append(
+            send(
+                p_ref.at[place(opposite, c)],
+                given.at[pl.ds(c * step, step)],
+                near_out.at[c],
+                near_in.at[c],
+                {"tensor": partner},
+            )
+        )
+        near[-1].start()
+    own = send(
+        p_ref.at[pl.ds(pl.multiple_of(partner * rows, rows), rows)],
+        own_in,
+        own_out,
+        own_sem,
+        {"tensor": partner},
+    )
+    own.start()
+    for c in range(chunks):
+        near[c].wait_recv()
+        part = pl.ds(c * step, step)
+        outgoing[part, :] = (
+            p_ref[place(across, c), :].astype(jnp.float32) + given[part, :].astype(jnp.float32)
+        ).astype(outgoing.dtype)
+        far.append(
+            send(
+                outgoing.at[part], arriving.at[part], far_out.at[c], far_in.at[c], {"tensor": across}
+            )
+        )
+        far[-1].start()
+    own.wait_recv()
+    for c in range(chunks):
+        far[c].wait_recv()
+        part = pl.ds(c * step, step)
+        o_ref[part, :] = (
+            p_ref[place(me, c), :].astype(jnp.float32)
+            + own_in[part, :].astype(jnp.float32)
+            + arriving[part, :].astype(jnp.float32)
+        )
+    own.wait_send()
+    for copy in near + far:
+        copy.wait_send()
+
+
+def tensor_scatter(values, number):
+    chunks = 4
+    rows, columns = values.shape[0] // 4, values.shape[1]
+    block = pltpu.VMEM((rows, columns), values.dtype)
+    return pl.pallas_call(
+        functools.partial(scatter_kernel, chunks),
+        in_specs=[pl.BlockSpec(memory_space=pltpu.VMEM)],
+        out_specs=pl.BlockSpec(memory_space=pltpu.VMEM),
+        out_shape=jax.ShapeDtypeStruct((rows, columns), jnp.float32),
+        scratch_shapes=[block] * 4
+        + [pltpu.SemaphoreType.DMA((chunks,))] * 2
+        + [pltpu.SemaphoreType.DMA(())] * 2
+        + [pltpu.SemaphoreType.DMA((chunks,))] * 2,
+        compiler_params=pltpu.CompilerParams(collective_id=number, has_side_effects=True),
+        cost_estimate=pl.CostEstimate(
+            flops=0, transcendentals=0, bytes_accessed=80 * rows * columns * 2
+        ),
+        name="tensor_scatter",
+    )(values)
+
+
+def sum_kernel(data_count, x_ref, o_ref, near_all, far_all, near_out, near_in, far_out, far_in):
+    me = lax.axis_index("tensor")
+    data = lax.axis_index("dp")
+    near_names = [{"tensor": lax.rem(me + k, 4)} for k in range(1, 4)]
+    far_names = [{"dp": lax.rem(data + k, data_count)} for k in range(1, data_count)]
+    greet(near_names + far_names)
+    copies = []
+    for k, name in enumerate(near_names):
+        copies.append(send(x_ref, near_all.at[me], near_out.at[k], near_in.at[k], name))
+        copies[-1].start()
+    near_all[me] = x_ref[...]
+    for copy in copies:
+        copy.wait()
+    o_ref[...] = near_all[0] + near_all[1] + near_all[2] + near_all[3]
+    copies = []
+    for k, name in enumerate(far_names):
+        copies.append(send(o_ref, far_all.at[data], far_out.at[k], far_in.at[k], name))
+        copies[-1].start()
+    far_all[data] = o_ref[...]
+    for copy in copies:
+        copy.wait()
+    o_ref[...] = jnp.sum(far_all[...], axis=0)
+
+
+def sum_all(values, number):
+    data_count = lax.axis_size("dp")
+    return pl.pallas_call(
+        functools.partial(sum_kernel, data_count),
+        in_specs=[pl.BlockSpec(memory_space=pltpu.VMEM)],
+        out_specs=pl.BlockSpec(memory_space=pltpu.VMEM),
+        out_shape=jax.ShapeDtypeStruct(values.shape, jnp.float32),
+        scratch_shapes=[
+            pltpu.VMEM((4,) + values.shape, jnp.float32),
+            pltpu.VMEM((data_count,) + values.shape, jnp.float32),
+            pltpu.SemaphoreType.DMA((3,)),
+            pltpu.SemaphoreType.DMA((3,)),
+            pltpu.SemaphoreType.DMA((data_count - 1,)),
+            pltpu.SemaphoreType.DMA((data_count - 1,)),
+        ],
+        compiler_params=pltpu.CompilerParams(collective_id=number, has_side_effects=True),
+        cost_estimate=pl.CostEstimate(flops=0, transcendentals=0, bytes_accessed=30_000_000),
+        name="sum_all",
+    )(values)
 
 
 def split_pieces(values):
@@ -433,7 +653,8 @@
         jnp.concatenate(pair_major(w_query, w_key, w_value, wide) + [small], axis=1), "dp"
     )
     second_full = gather(jnp.concatenate([w_outgate, w_output.T], axis=1), "dp")
-    third_full = gather(jnp.concatenate([w_gate, w_up, w_down.T], axis=1), "dp")
+    third_full = gather(jnp.concatenate([w_gate, w_up], axis=1), "dp")
+    down_turned = gather(w_down.T, "dp")
     qkv_full = first_full[:, : 3 * width]
     small_full = first_full[:, 3 * width :]
     gain_one = small_full[:, heads].astype(jnp.float32)
@@ -441,13 +662,13 @@
     outgate_full = second_full[:, :width]
     output_turned = second_full[:, width:]
     gate_full = third_full[:, :hidden_width]
-    up_full = third_full[:, hidden_width : 2 * hidden_width]
-    down_turned = third_full[:, 2 * hidden_width :]
-
+    up_full = third_full[:, hidden_width:]
+
+    tokens_all, out_grad_all = tensor_gather((tokens, out_grad), 0)
+    tokens_all_float = tokens_all.astype(jnp.float32)
+    normed_all = (tokens_all_float * rms_scale(tokens_all_float) * gain_one).astype(jnp.bfloat16)
     rows_float = tokens.astype(jnp.float32)
     scale_one = rms_scale(rows_float)
-    normed_low = (rows_float * scale_one * gain_one).astype(jnp.bfloat16)
-    normed_all = gather(normed_low, "tensor")
     projected = nn(normed_all, first_full)
     gate_logit = nn(normed_all, outgate_full)
     bias_local = lax.dynamic_slice_in_dim(forget_bias, tensor_index * heads, heads, 0)
@@ -461,11 +682,11 @@
     )
     gate_open = jax.nn.sigmoid(gate_logit)
     gated_low = (attended * gate_open).astype(jnp.bfloat16)
-    mixed = rows_float + scatter(nt(gated_low, output_turned), "tensor")
+    mixed = rows_float + tensor_scatter(nt(gated_low, output_turned).astype(jnp.bfloat16), 1)
 
     scale_two = rms_scale(mixed)
     normed_mid = (mixed * scale_two * gain_two).astype(jnp.bfloat16)
-    mid_all = gather(normed_mid, "tensor")
+    mid_all = tensor_gather((normed_mid,), 2)[0]
     gate_value = nn(mid_all, gate_full)
     up_value = nn(mid_all, up_full)
     gate_sigmoid = jax.nn.sigmoid(gate_value)
@@ -475,22 +696,24 @@
 
     live_rows = tensor_index * local_rows + jnp.arange(local_rows) < length
     grad_out = jnp.where(live_rows[:, None], out_grad, jnp.zeros_like(out_grad))
-    grad_out_all = gather(grad_out, "tensor")
+    grad_out_all = jnp.where(
+        jnp.arange(slot)[:, None] < length, out_grad_all, jnp.zeros_like(out_grad_all)
+    )
     grad_hidden = nn(grad_out_all, down_turned)
     grad_down = tn(grad_out_all, hidden_low).astype(jnp.bfloat16)
     grad_gate_low = (
         grad_hidden * up_value * gate_sigmoid * (1.0 + gate_value * (1.0 - gate_sigmoid))
     ).astype(jnp.bfloat16)
     grad_up_low = (grad_hidden * gate_silu).astype(jnp.bfloat16)
-    grad_mid = scatter(nt(grad_gate_low, gate_full) + nt(grad_up_low, up_full), "tensor")
+    grad_mid = tensor_scatter(
+        (nt(grad_gate_low, gate_full) + nt(grad_up_low, up_full)).astype(jnp.bfloat16), 1
+    )
     grad_gate_w = tn(mid_all, grad_gate_low).astype(jnp.bfloat16)
     grad_up_w = tn(mid_all, grad_up_low).astype(jnp.bfloat16)
     grad_gain_two = jnp.sum(grad_mid * mixed * scale_two, axis=0)
     grad_mixed = grad_out.astype(jnp.float32) + norm_backward(mixed, scale_two, grad_mid * gain_two)
-    grad_mixed_all = gather(grad_mixed.astype(jnp.bfloat16), "tensor")
-    grad_third = jnp.concatenate([grad_gate_w, grad_up_w, grad_down], axis=1)
-    grad_third, grad_mixed_all = lax.optimization_barrier((grad_third, grad_mixed_all))
-    third_sum = scatter(grad_third, "dp")
+    grad_mixed_all = tensor_gather((grad_mixed.astype(jnp.bfloat16),), 2)[0]
+    third_sum = scatter(jnp.concatenate([grad_gate_w, grad_up_w, grad_down], axis=1), "dp")
 
     grad_output_w = tn(grad_mixed_all, gated_low).astype(jnp.bfloat16)
     grad_gated = nn(grad_mixed_all, output_turned)
@@ -514,11 +737,13 @@
     grad_forget_low = (grad_log_forget * jax.nn.sigmoid(-forget_logit)).astype(jnp.bfloat16)
     grad_forget_wide = jnp.pad(grad_forget_low, ((0, 0), (0, wide - heads)))
     grad_bias_local = jnp.sum(grad_forget_low.astype(jnp.float32), axis=0)
-    grad_normed = scatter(
-        nt(grad_qkv, qkv_full)
-        + nt(grad_gate_logit_low, outgate_full)
-        + nt(grad_forget_wide, small_full),
-        "tensor",
+    grad_normed = tensor_scatter(
+        (
+            nt(grad_qkv, qkv_full)
+            + nt(grad_gate_logit_low, outgate_full)
+            + nt(grad_forget_wide, small_full)
+        ).astype(jnp.bfloat16),
+        1,
     )
     grad_first = jnp.concatenate(
         [
@@ -535,10 +760,16 @@
     bias_spread = lax.dynamic_update_slice_in_dim(
         jnp.zeros(forget_bias.shape, jnp.float32), grad_bias_local, tensor_index * heads, 0
     )
-    gain_one_sum, gain_two_sum, query_sum, key_sum, bias_sum = lax.psum(
-        (grad_gain_one, grad_gain_two, gain_sums[0, :half], gain_sums[1, :half], bias_spread),
-        ("dp", "tensor"),
-    )
+    parts = (grad_gain_one, grad_gain_two, gain_sums[0, :half], gain_sums[1, :half], bias_spread)
+    joined = jnp.concatenate(parts)
+    lines = -(-joined.shape[0] // (8 * wide)) * 8
+    joined = jnp.pad(joined, (0, lines * wide - joined.shape[0])).reshape(lines, wide)
+    joined = sum_all(joined, 3).reshape(-1)
+    sums, start = [], 0
+    for part in parts:
+        sums.append(joined[start : start + part.shape[0]])
+        start += part.shape[0]
+    gain_one_sum, gain_two_sum, query_sum, key_sum, bias_sum = sums
     own = data_index * shard
     grad_query_w, grad_key_w, grad_value_w = from_pair_major(first_sum[:, : 3 * width], wide)
     after = 3 * width + wide

time: 1220 us -> 761 us (0.62)
  waiting for transfers between devices: 743 us -> 20.5 us
  Pallas kernels: 107 us -> 404 us
  blocking collectives: 40.5 us -> 0 us
    all_gather x7 -> x4, waiting for transfers between devices: 346 us -> 12.2 us  [gather(): return lax.all_gather(values, axis_name, axis=0, tiled=True)]
    pallas_call x0 -> x7, Pallas kernels: none -> 297 us  [the longest x3 155 us: tensor_gather(): pl.pallas_call(functools.partial(gather_kernel, count, chunks), in_specs=...]
    unnamed x15 -> x9, waiting for transfers between devices: 217 us -> 8.27 us
    reduce_scatter x4 -> x1, waiting for transfers between devices: 180 us -> 0.02 us  [scatter(): lax.psum_scatter(values.astype(jnp.bfloat16), axis_name, scatter_dimensio...]
    psum x1 -> x0, blocking collectives: 40.5 us -> none  [per_device(): lax.psum((grad_gain_one, grad_gain_two, gain_sums[0, :half], gain_sums[1,...]
    unnamed x119 -> x105, local copies, waits for them, and re-layouts: 44.5 us -> 43.6 us
  transfers between devices with their start and end apart: 13 -> 7, of which waited for: 12 -> 2; matrix products, arithmetic and copies ran while one was open for 13% -> 35% of each run, Pallas kernels for 3% -> 54%
where the time goes in v2:
time: 761 us; the launch traced here: 753 us
  Pallas kernels  404 us (53%)
  matrix products  195 us (26%)
  local copies, waits for them, and re-layouts  67.4 us (9%)
  other arithmetic  50.1 us (7%)
  waiting for transfers between devices  20.5 us (3%)
  between operations  15.8 us (2%)
    pallas_call x3, Pallas kernels, tensor_gather(): pl.pallas_call(functools.partial(gather_kernel, count, chunks), in_specs=...  155 us
    pallas_call x3, Pallas kernels, tensor_scatter(): pl.pallas_call(functools.partial(scatter_kernel, chunks), in_specs=[pl.Bl...  130 us
    dot_general x6, matrix products, nn(): return jnp.dot(left, right, preferred_element_type=jnp.float32)  73.6 us
    dot_general x7, matrix products, nt(): lax.dot_general(left, right, (((1,), (1,)), ((), ())), preferred_element_...  72.9 us
    pallas_call x1, Pallas kernels, attend_back(): pl.pallas_call(functools.partial(attend_back_kernel, half, block), grid=(...  72.1 us
    dot_general x7, matrix products, tn(): lax.dot_general(left, right, (((0,), (0,)), ((), ())), preferred_element_...  48.8 us
    unnamed x105, local copies, waits for them, and re-layouts  43.6 us
    pallas_call x1, Pallas kernels, attend(): pl.pallas_call(functools.partial(attend_kernel, heads, half, block), grid...  34.5 us
  transfers between devices with their start and end apart: 7, of which 2 were waited for; matrix products, arithmetic and copies ran while one was open for 35% of the time, Pallas kernels for 54%

profile of v2, /device:TPU:0, one launch (start us, length us, event | category | flops | bytes accessed | tf_op | source)
XLA Modules:
  0.0 753.4 jit_solution(5104533174330687111)
XLA Ops:
  12.4 1.7 pad_maximum_fusion.6
  14.2 2.1 pad_maximum_fusion.2
  17.0 75.8 %tensor_gather.3 = (bf16[2048,1536]{1,0:T(8,128)(2,1)}, bf16[2048,1536]{1,0:T(8,128)(2,1)}) custom-call(bf16[512,1536]{1,0:T(8,128)(2,1)} %refs_0_.1, bf16[512,1536]{1,0:T(8,128)(2,1)} %refs_1_.1), custom_call_target="tpu_custom_call" | custom-call | bytes 251658240 | tf_op jit(solution)/shard_map/tensor_gather/pallas_call | solution.py:414
  92.8 4.3 fusion
  99.2 1.7 convert_reduce_fusion.1
  100.9 11.7 %fusion.46.x_ref = f32[2048,1280]{1,0:T(8,128)S(1)} fusion(bf16[1536,1280]{1,0:T(8,128)(2,1)} %all-gather.5.cloned.1.call-done, bf16[2048,1536]{1,0:T(8,128)(2,1)} %get-tuple-element.24, f32[1536]{0:T(1024)S(1)} %get-tuple-element.101, f32[2048]{0:T(1024)S(1)} %add_rsqrt_fusion), kind=kOutput, calls=%fused_computation.119 | convolution fusion | flops 8065646592 | bytes 20723712 | tf_op jit(solution)/shard_map/dot_general | solution.py:28
  112.6 3.9 copy-done.11
  117.5 1.7 reduce-window.14
  120.0 1.4 fusion.23
  121.4 2.0 maximum_maximum_fusion.1
  123.4 34.5 %attend.1 = (f32[2048,384]{1,0:T(8,128)}, bf16[6,2048,128]{2,1,0:T(8,128)(2,1)}, bf16[6,2048,128]{2,1,0:T(8,128)(2,1)}) custom-call(f32[2048,1280]{1,0:T(8,128)} %copy-done.11, bf16[2048,128]{1,0:T(8,128)(2,1)} %get-tuple-element.155.cq_ref, bf16[2048,128]{1,0:T(8,128)(2,1)} %get-tuple-element.154.ck_ref, f32[1,128]{1,0:T(1,128)} %broadcast_in_dim_tile.6.qg_ref, ...), custom_call_target="tpu_custom_call" | custom-call | flops 8053063680 | bytes 18874368 | tf_op jit(solution)/shard_map/attend/pallas_call | solution.py:256
  158.0 9.7 %multiply_convert_fusion.6 = (bf16[2048,384]{1,0:T(8,128)(2,1)S(1)}, f32[2048,384]{1,0:T(8,128)}) fusion(f32[2048,384]{1,0:T(8,128)} %get-tuple-element.25.att_ref, bf16[1536,768]{1,0:T(8,128)(2,1)} %all-gather.7.cloned.1.call-done, bf16[2048,1536]{1,0:T(8,128)(2,1)} %get-tuple-element.24, f32[1536]{0:T(1024)S(1)} %get-tuple-element.101, ...), kind=kOutput, calls=%fused_computation.43 | convolution fusion | flops 2432434176 | bytes 15349760 | tf_op jit(solution)/shard_map/dot_general | solution.py:28
  167.6 1.2 copy-done.30
  168.8 5.9 convolution_convert_fusion.2.p_ref
  174.7 43.3 %tensor_scatter.3 = f32[512,1536]{1,0:T(8,128)} custom-call(bf16[2048,1536]{1,0:T(8,128)(2,1)} %convolution_convert_fusion.2.p_ref), custom_call_target="tpu_custom_call" | custom-call | bytes 125829120 | tf_op jit(solution)/shard_map/tensor_scatter/pallas_call | solution.py:492
  218.0 3.4 multiply_reduce_fusion.2
  222.1 1.1 copy-done
  223.2 1.5 multiply_convert_fusion.5.refs_0_
  224.6 39.6 %tensor_gather.4 = bf16[2048,1536]{1,0:T(8,128)(2,1)} custom-call(bf16[512,1536]{1,0:T(8,128)(2,1)} %multiply_convert_fusion.5.refs_0_), custom_call_target="tpu_custom_call" | custom-call | bytes 125829120 | tf_op jit(solution)/shard_map/tensor_gather/pallas_call | solution.py:414
  264.3 12.4 %fusion.14 = f32[2048,1024]{1,0:T(8,128)} fusion(bf16[2048,1536]{1,0:T(8,128)(2,1)} %tensor_gather.4, bf16[1536,2048]{1,0:T(8,128)(2,1)} %all-gather.9.cloned.1.call-done), kind=kOutput, calls=%fused_computation.49 | convolution fusion | flops 6442450944 | bytes 17825792 | tf_op jit(solution)/shard_map/dot_general | solution.py:28
  276.7 9.5 %fusion.18 = f32[2048,1024]{1,0:T(8,128)} fusion(bf16[2048,1536]{1,0:T(8,128)(2,1)S(1)} %copy-done.4, bf16[1536,2048]{1,0:T(8,128)(2,1)S(1)} %copy-done.25), kind=kOutput, calls=%fused_computation.53 | convolution fusion | flops 6442450944 | bytes 17825792 | tf_op jit(solution)/shard_map/dot_general | solution.py:28
  286.1 12.1 %all-gather.11.cloned.1.call-done = bf16[1536,1024]{1,0:T(8,128)(2,1)} async-done(((bf16[192,1024]{1,0:T(8,128)(2,1)}), bf16[1536,1024]{1,0:T(8,128)(2,1)}) %all-gather.11.cloned.1.call-update) | async-done | bytes 3145744 | tf_op jit(solution)/shard_map/all_gather | solution.py:585
  298.3 20.4 %multiply_convert_fusion = (bf16[2048,1024]{1,0:T(8,128)(2,1)}, bf16[2048,1024]{1,0:T(8,128)(2,1)}, bf16[2048,1024]{1,0:T(8,128)(2,1)S(1)}) fusion(f32[2048,1024]{1,0:T(8,128)} %fusion.18, f32[2048,1024]{1,0:T(8,128)} %fusion.14, bf16[1536,1024]{1,0:T(8,128)(2,1)} %all-gather.11.cloned.1.call-done, bf16[2048,1536]{1,0:T(8,128)(2,1)} %get-tuple-element.26, ...), kind=kOutput, calls=%fused_computation.8 | convolution fusion | flops 6477053952 | bytes 38799360 | tf_op jit(solution)/shard_map/dot_general | solution.py:28
  318.7 2.1 copy-done.33
  320.8 8.9 %convolution_convert_fusion.1 = bf16[2048,1536]{1,0:T(8,128)(2,1)} fusion(bf16[2048,1024]{1,0:T(8,128)(2,1)S(1)} %get-tuple-element.110, bf16[1536,1024]{1,0:T(8,128)(2,1)S(1)} %copy-done.26), kind=kOutput, calls=%fused_computation.14 | convolution fusion | flops 6445596672 | bytes 13631488 | tf_op jit(solution)/shard_map/dot_general | solution.py:16
  329.8 10.5 %convolution_convert_fusion.4 = bf16[1536,1024]{0,1:T(8,128)(2,1)S(1)} fusion(bf16[2048,1536]{1,0:T(8,128)(2,1)} %tensor_gather.4, bf16[2048,1024]{1,0:T(8,128)(2,1)} %get-tuple-element.108), kind=kOutput, calls=%fused_computation.24 | convolution fusion | flops 6444023808 | bytes 13631488 | tf_op jit(solution)/shard_map/dot_general | solution.py:22
  340.4 8.8 %convolution_convert_fusion.5 = bf16[1536,1024]{0,1:T(8,128)(2,1)S(1)} fusion(bf16[2048,1536]{1,0:T(8,128)(2,1)S(1)} %bitcast.85, bf16[2048,1024]{1,0:T(8,128)(2,1)} %get-tuple-element.109), kind=kOutput, calls=%fused_computation.25 | convolution fusion | flops 6444023808 | bytes 13631488 | tf_op jit(solution)/shard_map/dot_general | solution.py:22
  349.2 9.5 %convolution_convert_fusion.3 = bf16[1536,1024]{0,1:T(8,128)(2,1)S(1)} fusion(bf16[2048,1024]{1,0:T(8,128)(2,1)} %copy-done.33, bf16[2048,1536]{1,0:T(8,128)(2,1)S(1)} %bitcast.100, pred[2048]{0:T(1024)(128)(4,1)S(1)} %iota_compare_fusion), kind=kOutput, calls=%fused_computation.23 | convolution fusion | flops 6447169536 | bytes 13633536 | tf_op jit(solution)/shard_map/dot_general | solution.py:22
  358.7 4.3 pad_maximum_fusion
  363.1 12.7 %copy.107 = bf16[1536,3072]{1,0:T(8,128)(2,1)} copy(bf16[1536,3072]{0,1:T(8,128)(2,1)} %pad_maximum_fusion) | data formatting | bytes 18874368
  375.8 13.1 %fusion.16 = f32[2048,1536]{1,0:T(8,128)} fusion(bf16[2048,1024]{1,0:T(8,128)(2,1)} %get-tuple-element.109, bf16[1536,2048]{1,0:T(8,128)(2,1)} %all-gather.9.cloned.1.call-done), kind=kOutput, calls=%fused_computation.51 | convolution fusion | flops 6442450944 | bytes 19922944 | tf_op jit(solution)/shard_map/dot_general | solution.py:16
  388.9 11.7 %add_convert_fusion.1.p_ref = bf16[2048,1536]{1,0:T(8,128)(2,1)} fusion(f32[2048,1536]{1,0:T(8,128)} %fusion.16, bf16[2048,1024]{1,0:T(8,128)(2,1)S(1)} %copy-done.32, bf16[1536,2048]{1,0:T(8,128)(2,1)S(1)} %bitcast.98), kind=kOutput, calls=%fused_computation.6 | convolution fusion | flops 6448742400 | bytes 26214400 | tf_op jit(solution)/shard_map/dot_general | solution.py:16
  400.7 43.4 %tensor_scatter.4 = f32[512,1536]{1,0:T(8,128)} custom-call(bf16[2048,1536]{1,0:T(8,128)(2,1)} %add_convert_fusion.1.p_ref), custom_call_target="tpu_custom_call" | custom-call | bytes 125829120 | tf_op jit(solution)/shard_map/tensor_scatter/pallas_call | solution.py:492
  444.1 2.7 multiply_reduce_fusion
  446.8 5.2 fusion.48
  452.1 39.8 %tensor_gather.5 = bf16[2048,1536]{1,0:T(8,128)(2,1)} custom-call(bf16[512,1536]{1,0:T(8,128)(2,1)} %get-tuple-element.104.refs_0_), custom_call_target="tpu_custom_call" | custom-call | bytes 125829120 | tf_op jit(solution)/shard_map/tensor_gather/pallas_call | solution.py:414
  491.9 10.0 %multiply_convert_fusion.3 = (bf16[2048,384]{1,0:T(8,128)(2,1)}, bf16[2048,384]{1,0:T(8,128)(2,1)}) fusion(f32[2048,384]{1,0:T(8,128)} %get-tuple-element.157, f32[2048,384]{1,0:T(8,128)} %get-tuple-element.25.att_ref, bf16[2048,1536]{1,0:T(8,128)(2,1)} %tensor_gather.5, bf16[1536,768]{1,0:T(8,128)(2,1)S(1)} %copy-done.7), kind=kOutput, calls=%fused_computation.36 | convolution fusion | flops 2421424128 | bytes 16908288 | tf_op jit(solution)/shard_map/dot_general | solution.py:28
  501.9 72.1 %attend_back.1 = (bf16[2048,1152]{1,0:T(8,128)(2,1)}, f32[2048,128]{1,0:T(8,128)}, f32[8,128]{1,0:T(8,128)}) custom-call(f32[2048,1280]{1,0:T(8,128)} %copy-done.11, bf16[6,2048,128]{2,1,0:T(8,128)(2,1)} %get-tuple-element.27.qb_ref, bf16[6,2048,128]{2,1,0:T(8,128)(2,1)} %get-tuple-element.28.kf_ref, f32[2048,384]{1,0:T(8,128)} %get-tuple-element.25.att_ref, ...), custom_call_target="tpu_custom_call" | custom-call | flops 20132659200 | bytes 31457280 | tf_op jit(solution)/shard_map/attend_back/pallas_call | solution.py:295
  574.0 6.8 rev.6
  581.2 1.7 reduce-window.16
  584.1 1.7 convert_reduce_fusion
  585.9 4.9 convolution_convert_fusion.8
  590.9 2.7 convolution_convert_fusion.6
  593.6 3.0 convolution_convert_fusion.7
  596.6 9.4 %convolution_convert_fusion = bf16[1536,1152]{0,1:T(8,128)(2,1)S(1)} fusion(bf16[2048,1152]{1,0:T(8,128)(2,1)S(1)} %bitcast.102, bf16[2048,1536]{1,0:T(8,128)(2,1)S(1)} %bitcast.81, f32[1536]{0:T(1024)S(1)} %copy-done.16, f32[2048]{0:T(1024)S(1)} %copy-done.22), kind=kOutput, calls=%fused_computation.13 | convolution fusion | flops 7262109696 | bytes 14563328 | tf_op jit(solution)/shard_map/dot_general | solution.py:22
  606.1 3.1 pad_maximum_fusion.1
  609.1 8.7 %copy.105 = bf16[1536,2048]{1,0:T(8,128)(2,1)} copy(bf16[1536,2048]{0,1:T(8,128)(2,1)} %pad_maximum_fusion.1) | data formatting | bytes 12582912
  618.5 7.9 %fusion.32 = f32[2048,1536]{1,0:T(8,128)} fusion(bf16[2048,384]{1,0:T(8,128)(2,1)S(1)} %copy-done.5, bf16[1536,768]{1,0:T(8,128)(2,1)} %all-gather.7.cloned.1.call-done), kind=kOutput, calls=%fused_computation.80 | convolution fusion | flops 2415919104 | bytes 15335424 | tf_op jit(solution)/shard_map/dot_general | solution.py:16
  626.4 12.9 %fusion.4 = f32[2048,1536]{1,0:T(8,128)} fusion(bf16[2048,1152]{1,0:T(8,128)(2,1)} %get-tuple-element.29, bf16[1536,1280]{1,0:T(8,128)(2,1)S(1)} %copy-done.12), kind=kOutput, calls=%fused_computation.26 | convolution fusion | flops 7247757312 | bytes 20840448 | tf_op jit(solution)/shard_map/dot_general | solution.py:16
  639.4 12.4 %add_convert_fusion.p_ref = bf16[2048,1536]{1,0:T(8,128)(2,1)} fusion(f32[2048,1536]{1,0:T(8,128)} %fusion.4, f32[2048,1536]{1,0:T(8,128)} %fusion.32, bf16[2048,6]{1,0:T(8,128)(2,1)S(1)} %get-tuple-element.103, bf16[1536,1280]{1,0:T(8,128)(2,1)S(1)} %copy-done.12), kind=kOutput, calls=%fused_computation.5 | convolution fusion | flops 814743552 | bytes 32374784 | tf_op jit(solution)/shard_map/dot_general | solution.py:16
  651.7 43.3 %tensor_scatter.5 = f32[512,1536]{1,0:T(8,128)} custom-call(bf16[2048,1536]{1,0:T(8,128)(2,1)} %add_convert_fusion.p_ref), custom_call_target="tpu_custom_call" | custom-call | bytes 125829120 | tf_op jit(solution)/shard_map/tensor_scatter/pallas_call | solution.py:492
  696.4 3.5 fusion.12
  700.5 12.2 %sum_all.1 = f32[32,128]{1,0:T(8,128)} custom-call(f32[32,128]{1,0:T(8,128)} %pad_bitcast_fusion.x_ref), custom_call_target="tpu_custom_call" | custom-call | bytes 30000000 | tf_op jit(solution)/shard_map/sum_all/pallas_call | solution.py:535
  714.8 1.2 slice.222
  715.9 1.3 fusion.54
  717.3 4.8 fusion.9
  722.1 1.6 copy.108
  724.1 1.2 copy.103
  725.3 1.1 fusion.49
  726.4 2.4 copy.101
  728.9 1.2 copy.102
  730.1 7.6 %reduce-scatter.10.cloned.1.call-done = bf16[192,2048]{1,0:T(8,128)(2,1)} async-done(((bf16[1536,2048]{1,0:T(8,128)(2,1)}), bf16[192,2048]{1,0:T(8,128)(2,1)}) %reduce-scatter.10.cloned.1.call-update) | async-done | bytes 786448
  737.7 1.4 copy.106
  742.6 1.1 pad_maximum_fusion.4
  (169 shorter events, 22.6 us)
Async XLA Ops:
  7.2 92.0 %all-gather.5.cloned.1.call-start = ((), (), s32[]{:S(2)}) async-start(), calls=%async_computation.3 | async-start | bytes 4423680 | tf_op jit(solution)/shard_map/all_gather | solution.py:585
  12.4 145.5 %all-gather.7.cloned.1.call-start = ((), (), s32[]{:S(2)}) async-start(), calls=%async_computation.4 | async-start | bytes 2654208 | tf_op jit(solution)/shard_map/all_gather | solution.py:585
  14.2 250.0 %all-gather.9.cloned.1.call-start = ((), (), s32[]{:S(2)}) async-start(), calls=%async_computation.5 | async-start | bytes 7077888 | tf_op jit(solution)/shard_map/all_gather | solution.py:585
  16.3 282.0 %all-gather.11.cloned.1.call-start = ((), (), s32[]{:S(2)}) async-start(), calls=%async_computation.6 | async-start | bytes 3538944 | tf_op jit(solution)/shard_map/all_gather | solution.py:585
  16.9 429.9 %reduce-scatter.8.cloned.1.call-start = ((), (), s32[]{:S(2)}) async-start(), calls=%async_computation.7 | async-start | bytes 7864320 | tf_op jit(solution)/shard_map/reduce_scatter | solution.py:589
  17.0 80.9 %copy-start.27 = (bf16[64]{0:T(256)(128)(2,1)S(1)}, bf16[64]{0:T(256)(128)(2,1)}, u32[]{:S(2)}) copy-start(bf16[64]{0:T(256)(128)(2,1)} %param.26) | copy-start | bytes 388
  17.0 81.5 %copy-start.28 = (bf16[64]{0:T(256)(128)(2,1)S(1)}, bf16[64]{0:T(256)(128)(2,1)}, u32[]{:S(2)}) copy-start(bf16[64]{0:T(256)(128)(2,1)} %param.27) | copy-start | bytes 388
  17.0 82.1 %copy-start.29 = (f32[24]{0:T(128)S(1)}, f32[24]{0:T(128)}, u32[]{:S(2)}) copy-start(f32[24]{0:T(128)} %param.24) | copy-start | bytes 292
  97.1 60.8 %copy-start.21 = (f32[2048]{0:T(1024)}, f32[2048]{0:T(1024)S(1)}, u32[]{:S(2)}) copy-start(f32[2048]{0:T(1024)S(1)} %add_rsqrt_fusion) | copy-start | bytes 24580
  99.1 13.5 %copy-start.23 = (f32[6]{0:T(128)}, f32[6]{0:T(128)S(1)}, u32[]{:S(2)}) copy-start(f32[6]{0:T(128)S(1)} %dynamic_slice.10) | copy-start | bytes 76
  100.9 57.1 %copy-start.15 = (f32[1536]{0:T(1024)}, f32[1536]{0:T(1024)S(1)}, u32[]{:S(2)}) copy-start(f32[1536]{0:T(1024)S(1)} %get-tuple-element.101) | copy-start | bytes 18436
  100.9 121.2 %copy-start.13 = (f32[1536]{0:T(1024)}, f32[1536]{0:T(1024)S(1)}, u32[]{:S(2)}) copy-start(f32[1536]{0:T(1024)S(1)} %get-tuple-element.100) | copy-start | bytes 18436
  112.6 3.9 copy-start.11
  157.9 10.8 %copy-start.6 = (bf16[1536,768]{1,0:T(8,128)(2,1)S(1)}, bf16[1536,768]{1,0:T(8,128)(2,1)}, u32[]{:S(2)}) copy-start(bf16[1536,768]{1,0:T(8,128)(2,1)} %all-gather.7.cloned.1.call-done) | copy-start | bytes 7077892
  167.6 1.2 copy-start.30
  174.7 43.3 %copy-start.3 = (bf16[512,1536]{1,0:T(8,128)(2,1)S(1)}, bf16[512,1536]{1,0:T(8,128)(2,1)}, u32[]{:S(2)}) copy-start(bf16[512,1536]{1,0:T(8,128)(2,1)} %refs_0_.1) | copy-start | bytes 4718596
  221.4 1.7 copy-start
  222.1 1.1 copy-start.17
  264.2 12.4 %copy-start.4 = (bf16[2048,1536]{1,0:T(8,128)(2,1)S(1)}, bf16[2048,1536]{1,0:T(8,128)(2,1)}, u32[]{:S(2)}) copy-start(bf16[2048,1536]{1,0:T(8,128)(2,1)} %tensor_gather.4) | copy-start | bytes 18874372
  264.2 12.4 %copy-start.25 = (bf16[1536,2048]{1,0:T(8,128)(2,1)S(1)}, bf16[1536,2048]{1,0:T(8,128)(2,1)}, u32[]{:S(2)}) copy-start(bf16[1536,2048]{1,0:T(8,128)(2,1)} %all-gather.9.cloned.1.call-done) | copy-start | bytes 18874372
  298.3 22.5 %copy-start.26 = (bf16[1536,1024]{1,0:T(8,128)(2,1)S(1)}, bf16[1536,1024]{1,0:T(8,128)(2,1)}, u32[]{:S(2)}) copy-start(bf16[1536,1024]{1,0:T(8,128)(2,1)} %all-gather.11.cloned.1.call-done) | copy-start | bytes 9437188
  318.7 2.1 copy-start.33
  329.7 10.6 %slice-start.4 = ((s8[6291456]{0:T(1024)(128)(4,1)}), s8[2097152]{0:T(1024)(128)(4,1)S(1)}, s32[]{:S(2)}) async-start(s8[6291456]{0:T(1024)(128)(4,1)} %bitcast.84), calls=%async_computation.14 | async-start | bytes 4194304
  329.7 392.4 %reduce-scatter.12.cloned.1.call-start = ((), (), s32[]{:S(2)}) async-start(), calls=%async_computation.9 | async-start | bytes 10616832
  329.8 10.6 %slice-start.5 = ((s8[6291456]{0:T(1024)(128)(4,1)}), s8[4194304]{0:T(1024)(128)(4,1)S(1)}, s32[]{:S(2)}) async-start(s8[6291456]{0:T(1024)(128)(4,1)} %bitcast.84), calls=%async_computation.15 | async-start | bytes 8388608
  329.8 19.4 %slice-start.8 = ((s8[6291456]{0:T(1024)(128)(4,1)}), s8[4194304]{0:T(1024)(128)(4,1)S(1)}, s32[]{:S(2)}) async-start(s8[6291456]{0:T(1024)(128)(4,1)} %bitcast.99), calls=%async_computation.18 | async-start | bytes 8388608
  340.3 8.9 %slice-start.9 = ((s8[6291456]{0:T(1024)(128)(4,1)}), s8[2097152]{0:T(1024)(128)(4,1)S(1)}, s32[]{:S(2)}) async-start(s8[6291456]{0:T(1024)(128)(4,1)} %bitcast.99), calls=%async_computation.19 | async-start | bytes 4194304
  375.7 13.2 %slice-start.6 = ((s8[6291456]{0:T(1024)(128)(4,1)}), s8[2097152]{0:T(1024)(128)(4,1)S(1)}, s32[]{:S(2)}) async-start(s8[6291456]{0:T(1024)(128)(4,1)} %bitcast.97), calls=%async_computation.16 | async-start | bytes 4194304
  375.7 362.0 %reduce-scatter.10.cloned.1.call-start = ((), (), s32[]{:S(2)}) async-start(), calls=%async_computation.8 | async-start | bytes 7077888
  375.8 13.1 %slice-start.7 = ((s8[6291456]{0:T(1024)(128)(4,1)}), s8[4194304]{0:T(1024)(128)(4,1)S(1)}, s32[]{:S(2)}) async-start(s8[6291456]{0:T(1024)(128)(4,1)} %bitcast.97), calls=%async_computation.17 | async-start | bytes 8388608
  375.8 13.1 %copy-start.32 = (bf16[2048,1024]{1,0:T(8,128)(2,1)S(1)}, bf16[2048,1024]{1,0:T(8,128)(2,1)}, u32[]{:S(2)}) copy-start(bf16[2048,1024]{1,0:T(8,128)(2,1)} %get-tuple-element.108) | copy-start | bytes 12582916
  400.7 43.4 %copy-start.1 = (f32[512,1536]{1,0:T(8,128)S(1)}, f32[512,1536]{1,0:T(8,128)}, u32[]{:S(2)}) copy-start(f32[512,1536]{1,0:T(8,128)} %copy-done) | copy-start | bytes 9437188
  400.7 43.4 %copy-start.14 = (f32[1536]{0:T(1024)S(1)}, f32[1536]{0:T(1024)}, u32[]{:S(2)}) copy-start(f32[1536]{0:T(1024)} %copy-done.13) | copy-start | bytes 18436
  400.7 43.4 %copy-start.18 = (f32[512]{0:T(512)S(1)}, f32[512]{0:T(512)}, u32[]{:S(2)}) copy-start(f32[512]{0:T(512)} %copy-done.17) | copy-start | bytes 6148
  444.1 2.7 copy-start.20
  452.1 39.8 %copy-start.7 = (bf16[1536,768]{1,0:T(8,128)(2,1)S(1)}, bf16[1536,768]{1,0:T(8,128)(2,1)}, u32[]{:S(2)}) copy-start(bf16[1536,768]{1,0:T(8,128)(2,1)} %all-gather.7.cloned.1.call-done) | copy-start | bytes 7077892
  574.0 10.1 %copy-start.24 = (f32[6]{0:T(128)S(1)}, f32[6]{0:T(128)}, u32[]{:S(2)}) copy-start(f32[6]{0:T(128)} %copy-done.23) | copy-start | bytes 76
  574.0 11.9 %copy-start.16 = (f32[1536]{0:T(1024)S(1)}, f32[1536]{0:T(1024)}, u32[]{:S(2)}) copy-start(f32[1536]{0:T(1024)} %copy-done.15) | copy-start | bytes 18436
  574.0 11.8 %copy-start.22 = (f32[2048]{0:T(1024)S(1)}, f32[2048]{0:T(1024)}, u32[]{:S(2)}) copy-start(f32[2048]{0:T(1024)} %copy-done.21) | copy-start | bytes 24580
  584.1 6.7 slice-start.2
  585.8 5.0 slice-start.3
  585.9 5.0 copy-start.31
  585.9 7.7 %slice-start = ((s8[6291456]{0:T(1024)(128)(4,1)}), s8[4194304]{0:T(1024)(128)(4,1)S(1)}, s32[]{:S(2)}) async-start(s8[6291456]{0:T(1024)(128)(4,1)} %bitcast.80), calls=%async_computation.10 | async-start | bytes 8388608
  590.9 2.7 slice-start.1
  590.9 2.7 copy-start.5
  590.9 5.7 slice-start.10
  593.6 3.0 slice-start.11
  617.8 0.7 copy-start.19
  618.5 7.9 %copy-start.12 = (bf16[1536,1280]{1,0:T(8,128)(2,1)S(1)}, bf16[1536,1280]{1,0:T(8,128)(2,1)}, u32[]{:S(2)}) copy-start(bf16[1536,1280]{1,0:T(8,128)(2,1)} %all-gather.5.cloned.1.call-done) | copy-start | bytes 11796484
  695.0 22.2 %copy-start.2 = (f32[512,1536]{1,0:T(8,128)S(1)}, f32[512,1536]{1,0:T(8,128)}, u32[]{:S(2)}) copy-start(f32[512,1536]{1,0:T(8,128)} %tensor_scatter.5) | copy-start | bytes 9437188
  740.8 3.7 copy-start.8
  740.9 3.7 copy-start.9
  740.9 3.7 copy-start.10
Sparse Core Ops, SparseCore 0:
  12.5 72.1 all-gather.4
  87.5 50.4 all-gather.6
  140.8 97.2 all-gather.8
  240.0 58.1 all-gather.10
  329.8 57.5 reduce-scatter.7
  390.8 162.0 reduce-scatter.11
  618.0 119.7 reduce-scatter.9
